TPU v7x, 32 devices: a whole 2x2x4 slice. The times are simulated.
32 devices in a mesh: grp: 2 (over y), kvp: 4 (over z), tp: 4 (over x, core).
Axes of the slice: x: 2, y: 2, z: 4, core: 2. Of those that a mesh axis runs over, the one named last changes fastest.
Arguments:
- queries: bfloat16 [32, 4096], P('grp', 'tp'), parts along dimension 0, may hold values from -6 to 6
- keys: bfloat16 [32, 512, 512], P('grp', 'kvp', 'tp'), parts along dimension 0, may hold values from -6 to 6
- values: bfloat16 [32, 512, 512], P('grp', 'kvp', 'tp'), parts along dimension 0, may hold values from -6 to 6
- lengths: int32 [32], P('grp'), parts along dimension 0, may hold values from 256 to 512, as said below
- out_weight: bfloat16 [4096, 1536], P('tp', 'kvp'), may hold values from -0.375 to 0.375
- residual: bfloat16 [32, 1536], P('grp', 'kvp'), parts along dimension 0, may hold values from -20 to 20
- norm_gain: bfloat16 [1536], P('kvp'), may hold values from 0.099609375 to 1.8984375
- expert_ids: int32 [32, 4], P('grp'), parts along dimension 0, may hold values from 0 to 3, as said below
- gate_probs: float32 [32, 4], P('grp'), parts along dimension 0, may hold values from 0.2 to 1
- w_gate: bfloat16 [4, 1536, 1536], P('kvp', None, 'tp'), may hold values from -0.15625 to 0.15625
- w_up: bfloat16 [4, 1536, 1536], P('kvp', None, 'tp'), may hold values from -0.15625 to 0.15625
- w_down: bfloat16 [4, 1536, 1536], P('kvp', 'tp'), may hold values from -0.15625 to 0.15625
Outputs:
- attended: float32 [32, 4096], P('grp', 'tp'), parts along dimension 0
- mixed: bfloat16 [32, 1536], P('grp', 'kvp'), parts along dimension 0
There are 2 independent parts, one for each index of `grp`. A program takes and returns all parts, laid end to end along the dimension named above; an argument that names none is the same for every part. Nothing has to cross between parts.
Inputs may be any that keep to these rules, and one draw needn't show every extreme that they name: `lengths`: at least one sequence has all 512 positions valid. `expert_ids`: each row names 4 different experts; no expert is named by more than 16 rows, and some expert by exactly 16.
All inputs are finite; a program needn't handle non-finite values.
Results may differ from a plain program's by a relative error of at most 0.006.
Values may be sent and summed in bfloat16 or wider, within the bound.
No kernel may reach another device: no remote copies, remote signals or barrier semaphores. Data moves between devices by JAX's collectives and lax.ppermute only.
A program may use at most 64 MiB of HBM per device.

v0:
```python
import jax
import jax.numpy as jnp
from jax import lax
from jax.sharding import PartitionSpec as P

D = 1536
HEAD = 64


EPSILON = 1e-05
NEGATIVE = -1e30


def merged(part, axis, combine):
    gathered = jax.tree.map(lambda a: lax.all_gather(a, axis), part)

    def take(source):
        return jax.tree.map(lambda a: lax.dynamic_index_in_dim(a, source, 0, False), gathered)

    return lax.fori_loop(
        1, lax.axis_size(axis), lambda source, state: combine(state, take(source)), take(0)
    )


def slot_tables(expert_ids, gate_probs, experts, capacity):
    batch_size, top_count = expert_ids.shape
    flat_ids = expert_ids.reshape(-1)
    pair_count = flat_ids.shape[0]
    pair_order = jnp.arange(pair_count, dtype=jnp.int32)
    earlier_same = (flat_ids[:, None] == flat_ids[None, :]) & (
        pair_order[None, :] < pair_order[:, None]
    )
    slot_index = jnp.sum(earlier_same.astype(jnp.int32), axis=1)
    target_col = flat_ids * capacity + slot_index
    columns = jnp.arange(experts * capacity, dtype=jnp.int32)
    hit_table = (target_col[:, None] == columns[None, :]).astype(jnp.float32)
    hit_table = hit_table.reshape(batch_size, top_count, experts * capacity)
    dispatch = jnp.sum(hit_table, axis=1)
    combine = jnp.sum(hit_table * gate_probs[:, :, None], axis=1)
    return (dispatch, combine)


def merge_partial(earlier, latest):
    global_max = jnp.maximum(earlier[0], latest[0])
    lead_scale = jnp.exp(earlier[0] - global_max)
    trail_scale = jnp.exp(latest[0] - global_max)
    return (
        global_max,
        lead_scale * earlier[1] + trail_scale * latest[1],
        lead_scale[..., None] * earlier[2] + trail_scale[..., None] * latest[2],
    )


def on_device(
    queries,
    keys,
    values,
    lengths,
    out_weight,
    residual,
    norm_gain,
    expert_ids,
    gate_probs,
    w_gate,
    w_up,
    w_down,
):
    batch_size = queries.shape[0]
    local_kv = keys.shape[2] // HEAD
    local_heads = queries.shape[1] // HEAD
    group_size = local_heads // local_kv
    ctx_dev = keys.shape[1]
    shards = lax.axis_size("kvp")
    query_heads = queries.reshape(batch_size, local_kv, group_size, HEAD)
    key_rows = keys.reshape(batch_size, ctx_dev, local_kv, HEAD)
    value_rows = values.reshape(batch_size, ctx_dev, local_kv, HEAD)
    scores = jnp.einsum(
        "bgrd,bcgd->bgrc", query_heads, key_rows, preferred_element_type=jnp.float32
    ) * HEAD ** (-0.5)
    position = lax.axis_index("kvp") * ctx_dev + jnp.arange(ctx_dev, dtype=jnp.int32)
    valid_key = (position[None, :] < lengths[:, None])[:, None, None, :]
    masked = jnp.where(valid_key, scores, NEGATIVE)
    block_max = jnp.max(masked, axis=3)
    weights = jnp.where(valid_key, jnp.exp(masked - block_max[..., None]), 0.0)
    rounded = weights.astype(jnp.bfloat16)
    block_sum = jnp.sum(rounded.astype(jnp.float32), axis=3)
    block_out = jnp.einsum(
        "bgrc,bcgd->bgrd", rounded, value_rows, preferred_element_type=jnp.float32
    )
    global_max, denominator, summed = merged(
        (block_max, block_sum, block_out), "kvp", merge_partial
    )
    attended = (summed / denominator[..., None]).reshape(batch_size, local_heads * HEAD)
    projected = lax.psum(
        jnp.dot(attended.astype(jnp.bfloat16), out_weight, preferred_element_type=jnp.float32), "tp"
    )
    hidden_state = lax.optimization_barrier(
        (projected + residual.astype(jnp.float32)).astype(jnp.bfloat16)
    )
    state_wide = hidden_state.astype(jnp.float32)
    col_count = hidden_state.shape[1]
    exp_dev = w_gate.shape[0]
    experts = exp_dev * shards
    capacity = min(batch_size, max(2, 2 * batch_size * expert_ids.shape[1] // experts))
    dispatch, combine = slot_tables(expert_ids, gate_probs, experts, capacity)
    total_sq = lax.psum(jnp.sum(state_wide * state_wide, axis=1), "kvp")
    inverse = lax.rsqrt(total_sq / D + EPSILON)
    normed = (state_wide * inverse[:, None] * norm_gain.astype(jnp.float32)[None, :]).astype(
        jnp.bfloat16
    )
    outgoing = jnp.dot(
        dispatch.T.astype(jnp.bfloat16), normed, preferred_element_type=jnp.float32
    ).astype(jnp.bfloat16)
    outgoing = outgoing.reshape(experts, capacity, col_count)
    expert_rows = lax.all_to_all(outgoing, "kvp", split_axis=0, concat_axis=2, tiled=True)
    gate_proj = jnp.einsum("ecd,edf->ecf", expert_rows, w_gate, preferred_element_type=jnp.float32)
    up_proj = jnp.einsum("ecd,edf->ecf", expert_rows, w_up, preferred_element_type=jnp.float32)
    activation = (jax.nn.silu(gate_proj) * up_proj).astype(jnp.bfloat16)
    partial_value = jnp.einsum(
        "ecf,efd->ecd", activation, w_down, preferred_element_type=jnp.float32
    )
    returned = lax.all_to_all(partial_value, "kvp", split_axis=2, concat_axis=0, tiled=True)
    moe_local = jnp.dot(
        combine, returned.reshape(experts * capacity, col_count), precision=lax.Precision.HIGHEST
    )
    moe_term = lax.psum(moe_local, "tp")
    mixed = (state_wide + moe_term).astype(jnp.bfloat16)
    return (attended, mixed)


def solution(mesh):
    return jax.shard_map(
        on_device,
        mesh=mesh,
        in_specs=(
            P("grp", "tp"),
            P("grp", "kvp", "tp"),
            P("grp", "kvp", "tp"),
            P("grp"),
            P("tp", "kvp"),
            P("grp", "kvp"),
            P("kvp"),
            P("grp", None),
            P("grp", None),
            P("kvp", None, "tp"),
            P("kvp", None, "tp"),
            P("kvp", "tp", None),
        ),
        out_specs=(P("grp", "tp"), P("grp", "kvp")),
        check_vma=False,
    )
```

profile of v0, /device:TPU:0, one launch (start us, length us, event | category | flops | bytes accessed | tf_op | source)
XLA Modules:
  0.0 124.9 jit_solution(10427162739778779653)
XLA Ops:
  0.7 0.8 convert_element_type.54
  1.4 0.8 copy.99
  2.2 0.1 eq.13
  2.3 0.2 convert_reduce_fusion.2
  2.5 0.1 reduce_sum.49
  2.6 0.1 copy.100
  2.6 1.3 %multiply_add_fusion = s32[16,4]{0,1:T(4,128)} fusion(s32[16,4]{0,1:T(4,128)S(1)} %copy.100, s32[16,4]{0,1:T(4,128)} %param.21), kind=kLoop, calls=%fused_computation.48 | loop fusion | flops 128 | bytes 768 | tf_op jit(solution)/shard_map/add | solution.py:34
  3.9 0.9 reshape.104
  4.8 1.4 %copy.90 = bf16[16,128,128]{1,2,0:T(8,128)(2,1)S(1)} copy(bf16[16,128,128]{2,1,0:T(8,128)(2,1)} %param.15) | data formatting | bytes 1048576 | tf_op args[1]
  6.3 0.3 fusion.39
  6.6 14.9 %all-gather = f32[64,2,8]{2,1,0:T(2,128)S(1)} all-gather(f32[16,2,8]{2,1,0:T(2,128)S(1)} %get-tuple-element.236), channel_id=2, replica_groups=mesh['grp'=2,'kvp'=4,'tp'=4] {'kvp'}, dimensions={0}, use_global_device_ids=true | all-gather | bytes 5120 | tf_op jit(solution)/shard_map/all_gather | solution.py:15
  21.5 0.2 convert_reduce_fusion
  21.7 13.3 %all-gather.1 = f32[64,2,8]{2,1,0:T(2,128)S(1)} all-gather(f32[16,2,8]{2,1,0:T(2,128)S(1)} %convert_reduce_fusion), channel_id=3, replica_groups=mesh['grp'=2,'kvp'=4,'tp'=4] {'kvp'}, dimensions={0}, use_global_device_ids=true | all-gather | bytes 5120 | tf_op jit(solution)/shard_map/all_gather | solution.py:15
  35.1 0.1 copy.97
  35.3 0.1 copy.96
  35.4 0.3 copy.91
  35.7 0.4 fusion.35
  36.1 15.1 %all-gather.2 = f32[64,2,8,64]{3,2,1,0:T(8,128)S(1)} all-gather(f32[16,2,8,64]{3,2,1,0:T(8,128)S(1)} %fusion.35), channel_id=4, replica_groups=mesh['grp'=2,'kvp'=4,'tp'=4] {'kvp'}, dimensions={0}, use_global_device_ids=true | all-gather | bytes 327680 | tf_op jit(solution)/shard_map/all_gather | solution.py:15
  51.3 1.1 while.19
  51.3 0.1 copy.113
  51.5 0.2 fusion.53
  51.9 0.2 fusion.53
  52.2 0.2 fusion.53
  52.4 0.1 copy.98
  52.5 0.1 broadcast_divide_fusion
  52.6 0.7 reshape.107
  53.4 2.1 %fusion.18 = f32[16,384]{1,0:T(8,128)} fusion(bf16[1024,384]{1,0:T(8,128)(2,1)} %param.18, f32[16,1024]{1,0:T(8,128)} %reshape.107), kind=kOutput, calls=%fused_computation.30 | convolution fusion | flops 12599296 | bytes 876544 | tf_op jit(solution)/shard_map/dot_general | solution.py:95
  55.4 11.4 %psum.21 = f32[16,384]{1,0:T(8,128)} all-reduce(f32[16,384]{1,0:T(8,128)} %fusion.18), channel_id=1, replica_groups=mesh['grp'=2,'kvp'=4,'tp'=4] {'tp'}, use_global_device_ids=true, to_apply=%region_4.5 | all-reduce | flops 6144 | bytes 49152 | tf_op jit(solution)/shard_map/psum | solution.py:94
  66.8 0.7 add_convert_fusion
  67.5 0.6 fusion.21
  68.2 12.5 %psum.22 = f32[16]{0:T(128)} all-reduce(f32[16]{0:T(128)} %fusion.21), channel_id=1, replica_groups=mesh['grp'=2,'kvp'=4,'tp'=4] {'kvp'}, use_global_device_ids=true, to_apply=%region_9.10 | all-reduce | flops 16 | bytes 128 | tf_op jit(solution)/shard_map/psum | solution.py:106
  80.7 0.7 add_rsqrt_fusion
  81.4 1.4 %convert_reduce_fusion.1 = (bf16[16,64]{1,0:T(8,128)(2,1)S(1)}, f32[16,64]{1,0:T(8,128)}) fusion(s32[16,4]{0,1:T(4,128)} %multiply_add_fusion, f32[16,4]{0,1:T(4,128)} %param.22), kind=kLoop, calls=%fused_computation.25 | loop fusion | flops 18432 | bytes 6656 | tf_op jit(solution)/shard_map/reduce_sum | solution.py:38
  82.7 0.2 convolution_convert_fusion
  82.9 8.1 %all_to_all.30 = bf16[4,16,384]{2,1,0:T(8,128)(2,1)S(1)} all-to-all(bf16[4,16,384]{2,1,0:T(8,128)(2,1)S(1)} %bitcast.73), channel_id=1, replica_groups=mesh['grp'=2,'kvp'=4,'tp'=4] {'kvp'}, dimensions={0} | all-to-all | bytes 98304 | tf_op jit(solution)/shard_map/all_to_all | solution.py:115
  91.0 0.6 copy.110
  91.6 1.7 %fusion.7 = f32[16,384]{1,0:T(8,128)} fusion(bf16[16,1536]{1,0:T(8,128)(2,1)} %bitcast.23, bf16[1,1536,384]{2,1,0:T(8,128)(2,1)S(1)} %copy-done.2), kind=kOutput, calls=%fused_computation.12 | convolution fusion | flops 18874368 | bytes 1253376 | tf_op jit(solution)/shard_map/ecd,edf->ecf/dot_general | solution.py:116
  93.3 1.6 %fusion.3 = f32[16,1536]{0,1:T(8,128)S(1)} fusion(bf16[1,384,1536]{2,1,0:T(8,128)(2,1)S(1)} %copy-done, bf16[16,1536]{1,0:T(8,128)(2,1)} %bitcast.23, bf16[1,1536,384]{2,1,0:T(8,128)(2,1)S(1)} %copy-done.1, f32[16,384]{1,0:T(8,128)} %fusion.7), kind=kOutput, calls=%fused_computation.8 | convolution fusion | flops 37785600 | bytes 2531328 | tf_op jit(solution)/shard_map/ecf,efd->ecd/dot_general | solution.py:119
  95.0 0.6 broadcast.55
  95.6 7.2 %reduce = f32[1536,16]{1,0:T(8,128)S(1)} reduce(f32[1536,1,16]{2,1,0:T(1,128)S(1)} %bitcast.66, f32[]{:T(128)} %broadcast.55), dimensions={1}, to_apply=%bitcast.47.reduce_sub_computation | reduce | bytes 196612
  102.8 0.3 reshape.123
  103.1 8.2 %all_to_all.31 = f32[4,1,6144]{2,1,0:T(1,128)S(1)} all-to-all(f32[4,1,6144]{2,1,0:T(1,128)S(1)} %reshape.123), channel_id=1, replica_groups=mesh['grp'=2,'kvp'=4,'tp'=4] {'kvp'}, dimensions={0} | all-to-all | bytes 196608 | tf_op jit(solution)/shard_map/all_to_all | solution.py:122
  111.3 0.9 reduce.1
  112.3 1.3 %reshape.124 = f32[1536,1,16]{2,1,0:T(1,128)S(1)} reshape(f32[4,6144]{1,0:T(4,128)S(1)} %reduce.1) | data formatting | bytes 196608
  113.6 0.2 copy.109
  113.9 0.2 fusion.40
  114.0 10.3 %psum.23 = f32[16,384]{1,0:T(8,128)S(1)} all-reduce(f32[16,384]{1,0:T(8,128)S(1)} %fusion.40), channel_id=1, replica_groups=mesh['grp'=2,'kvp'=4,'tp'=4] {'tp'}, use_global_device_ids=true, to_apply=%region_10.11 | all-reduce | flops 6144 | bytes 49152 | tf_op jit(solution)/shard_map/psum | solution.py:126
  124.3 0.6 fusion.24
  (29 shorter events, 0.8 us)
Async XLA Ops:
  0.6 92.7 %copy-start = (bf16[1,384,1536]{2,1,0:T(8,128)(2,1)S(1)}, bf16[1,384,1536]{2,1,0:T(8,128)(2,1)}, u32[]{:S(2)}) copy-start(bf16[1,384,1536]{2,1,0:T(8,128)(2,1)} %param.25) | copy-start | bytes 3538948
  0.6 5.5 %copy-start.5 = (s32[16]{0:T(128)S(1)}, s32[16]{0:T(128)}, u32[]{:S(2)}) copy-start(s32[16]{0:T(128)} %param.17) | copy-start | bytes 196
  4.8 30.6 %copy-start.3 = (bf16[16,128,128]{2,1,0:T(8,128)(2,1)S(1)}, bf16[16,128,128]{2,1,0:T(8,128)(2,1)}, u32[]{:S(2)}) copy-start(bf16[16,128,128]{2,1,0:T(8,128)(2,1)} %param.16) | copy-start | bytes 1572868
  52.4 39.2 %copy-start.2 = (bf16[1,1536,384]{2,1,0:T(8,128)(2,1)S(1)}, bf16[1,1536,384]{2,1,0:T(8,128)(2,1)}, u32[]{:S(2)}) copy-start(bf16[1,1536,384]{2,1,0:T(8,128)(2,1)} %param.23) | copy-start | bytes 3538948
  53.4 40.0 %copy-start.1 = (bf16[1,1536,384]{2,1,0:T(8,128)(2,1)S(1)}, bf16[1,1536,384]{2,1,0:T(8,128)(2,1)}, u32[]{:S(2)}) copy-start(bf16[1,1536,384]{2,1,0:T(8,128)(2,1)} %param.24) | copy-start | bytes 3538948
  103.1 10.8 %copy-start.4 = (f32[16,64]{1,0:T(8,128)S(1)}, f32[16,64]{1,0:T(8,128)}, u32[]{:S(2)}) copy-start(f32[16,64]{1,0:T(8,128)} %get-tuple-element.217) | copy-start | bytes 12292
where the time goes:
time: 126 us; the launch traced here: 125 us
  blocking collectives  93.8 us (74%)
  other arithmetic  15.3 us (12%)
  local copies, waits for them, and re-layouts  8.31 us (7%)
  matrix products  6.53 us (5%)
    all_gather x3, blocking collectives, merged(): gathered = jax.tree.map(lambda a: lax.all_gather(a, axis), part)  43.4 us
    psum x1, blocking collectives, on_device(): total_sq = lax.psum(jnp.sum(state_wide * state_wide, axis=1), 'kvp')  12.5 us
    psum x1, blocking collectives, on_device(): lax.psum(jnp.dot(attended.astype(jnp.bfloat16), out_weight, preferred_ele...  11.4 us
    psum x1, blocking collectives, on_device(): moe_term = lax.psum(moe_local, 'tp')  10.3 us
    all_to_all x1, blocking collectives, on_device(): lax.all_to_all(partial_value, 'kvp', split_axis=2, concat_axis=0, tiled=T...  8.21 us
    all_to_all x1, blocking collectives, on_device(): lax.all_to_all(outgoing, 'kvp', split_axis=0, concat_axis=2, tiled=True)  8.06 us
    unnamed x1, other arithmetic  7.21 us
    unnamed x19, local copies, waits for them, and re-layouts  5.3 us

commit v1 on v0

--- a/solution.py
+++ b/solution.py
@@ -1,14 +1,248 @@
+import functools
+
 import jax
 import jax.numpy as jnp
 from jax import lax
+from jax.experimental import pallas as pl
+from jax.experimental.pallas import tpu as pltpu
 from jax.sharding import PartitionSpec as P
 
-D = 1536
 HEAD = 64
-
-
+LANES = 128
 EPSILON = 1e-05
 NEGATIVE = -1e30
+F32 = jnp.float32
+BF16 = jnp.bfloat16
+VMEM = pl.BlockSpec(memory_space=pltpu.VMEM)
+SMEM = pl.BlockSpec(memory_space=pltpu.SMEM)
+ANY = pl.BlockSpec(memory_space=pl.ANY)
+
+
+def exchange(x, axis):
+    size = lax.axis_size(axis)
+    moved = [lax.ppermute(x, axis, [(i, i ^ s) for i in range(size)]) for s in range(size - 1, 0, -1)]
+    return [x] + moved[::-1]
+
+
+def pairwise(parts, add):
+    parts = list(parts)
+    while len(parts) > 1:
+        parts = [add(parts[i], parts[i + 1]) for i in range(0, len(parts), 2)]
+    return parts[0]
+
+
+def add(a, b):
+    return a + b
+
+
+def split3(x):
+    first = x.astype(BF16).astype(F32)
+    rest = x - first
+    second = rest.astype(BF16).astype(F32)
+    return first, second, (rest - second).astype(BF16).astype(F32)
+
+
+def attention_body(heads, kv, chunks, len_ref, q_ref, k_hbm, v_hbm, out_ref, k_buf, v_buf, rows, stats, sems):
+    batch, context = k_buf.shape[:2]
+    group = heads // kv
+    step = batch // chunks
+
+    def copy(source, target, which, c):
+        part = pl.ds(c * step, step)
+        return pltpu.make_async_copy(source.at[part], target.at[part], sems.at[which, c])
+
+    for c in range(chunks):
+        copy(k_hbm, k_buf, 0, c).start()
+    for c in range(chunks):
+        copy(v_hbm, v_buf, 1, c).start()
+    lane = lax.broadcasted_iota(jnp.int32, (batch, LANES), 1)
+    low = lane < HEAD
+    for h in range(heads):
+        wide = q_ref[:, (h // 2) * LANES : (h // 2 + 1) * LANES].astype(F32)
+        half = h // group
+        if h % 2 != half:
+            wide = pltpu.roll(wide, HEAD, 1)
+        rows[h * batch : (h + 1) * batch, :] = jnp.where(low if half == 0 else ~low, wide, 0.0)
+    base = lax.axis_index("kvp") * context
+    spot = lax.broadcasted_iota(jnp.int32, (heads, context), 1)
+    slot = lax.broadcasted_iota(jnp.int32, (heads, LANES), 1)
+    mine = slot % heads == lax.broadcasted_iota(jnp.int32, (heads, LANES), 0)
+    field = slot // heads
+    query = [rows[pl.ds(b, heads, stride=batch), :].astype(BF16) for b in range(batch)]
+    for b in range(batch):
+        if b % step == 0:
+            copy(k_hbm, k_buf, 0, b // step).wait()
+            copy(v_hbm, v_buf, 1, b // step).wait()
+        scores = lax.dot_general(
+            query[b], k_buf[b], (((1,), (1,)), ((), ())), preferred_element_type=F32
+        ) * HEAD ** (-0.5)
+        valid = spot < len_ref[b] - base
+        masked = jnp.where(valid, scores, NEGATIVE)
+        top = jnp.max(masked, axis=1, keepdims=True)
+        weights = jnp.where(valid, jnp.exp(masked - top), 0.0).astype(BF16)
+        total = jnp.sum(weights.astype(F32), axis=1, keepdims=True)
+        summed = jnp.dot(weights, v_buf[b], preferred_element_type=F32)
+        rows[b * heads : (b + 1) * heads, :] = jnp.where(total > 0.0, summed / jnp.where(total > 0.0, total, 1.0), 0.0)
+        value = jnp.zeros((heads, LANES), F32)
+        for i, term in enumerate(split3(top) + split3(total)):
+            value = jnp.where(mine & (field == i), jnp.broadcast_to(term, (heads, LANES)), value)
+        stats[b : b + 1, :] = jnp.sum(value, axis=0, keepdims=True)
+    for pair in range(heads // 2):
+        sides = []
+        for h in (2 * pair, 2 * pair + 1):
+            wide = rows[pl.ds(h, batch, stride=heads), :]
+            sides.append(pltpu.roll(wide, HEAD, 1) if h % 2 != h // group else wide)
+        out_ref[:, pair * LANES : (pair + 1) * LANES] = jnp.where(low, sides[0], sides[1]).astype(BF16)
+    out_ref[:, heads * HEAD :] = stats[...].astype(BF16)
+
+
+def attention(queries, keys, values, lengths):
+    batch, context, width = keys.shape
+    heads = queries.shape[1] // HEAD
+    chunks = 4
+    return pl.pallas_call(
+        functools.partial(attention_body, heads, width // HEAD, chunks),
+        out_shape=jax.ShapeDtypeStruct((batch, heads * HEAD + LANES), BF16),
+        in_specs=[SMEM, VMEM, ANY, ANY],
+        out_specs=VMEM,
+        scratch_shapes=[
+            pltpu.VMEM(keys.shape, BF16),
+            pltpu.VMEM(values.shape, BF16),
+            pltpu.VMEM((batch * heads, LANES), F32),
+            pltpu.VMEM((batch, LANES), F32),
+            pltpu.SemaphoreType.DMA((2, chunks)),
+        ],
+        name="attention",
+    )(lengths, queries, keys, values)
+
+
+def merge_body(heads, size, *refs):
+    parts, weight, attended_ref, out_ref = refs[:size], refs[size], refs[size + 1], refs[size + 2]
+    batch = parts[0].shape[0]
+    tops, totals = [], []
+    for part in parts:
+        stats = part[:, heads * HEAD :].astype(F32)
+        turned = [stats] + [pltpu.roll(stats, LANES - i * heads, 1) for i in range(1, 6)]
+        tops.append(turned[0] + turned[1] + turned[2])
+        totals.append(turned[3] + turned[4] + turned[5])
+    top = pairwise(tops, jnp.maximum)
+    shares = [jnp.exp(t - top) * s for t, s in zip(tops, totals)]
+    inverse = 1.0 / pairwise(shares, add)
+    shares = [s * inverse for s in shares]
+    low = lax.broadcasted_iota(jnp.int32, (batch, LANES), 1) < HEAD
+    wide = (batch, LANES)
+    pieces = []
+    for pair in range(heads // 2):
+        columns = slice(pair * LANES, (pair + 1) * LANES)
+        terms = []
+        for share, part in zip(shares, parts):
+            left = jnp.broadcast_to(share[:, 2 * pair : 2 * pair + 1], wide)
+            right = jnp.broadcast_to(share[:, 2 * pair + 1 : 2 * pair + 2], wide)
+            terms.append(jnp.where(low, left, right) * part[:, columns].astype(F32))
+        piece = pairwise(terms, add)
+        attended_ref[:, columns] = piece
+        pieces.append(piece.astype(BF16))
+    out_ref[...] = jnp.dot(jnp.concatenate(pieces, axis=1), weight[...], preferred_element_type=F32).astype(BF16)
+
+
+def merge(parts, weight):
+    batch = parts[0].shape[0]
+    inputs, columns = weight.shape
+    return pl.pallas_call(
+        functools.partial(merge_body, inputs // HEAD, len(parts)),
+        out_shape=(
+            jax.ShapeDtypeStruct((batch, inputs), F32),
+            jax.ShapeDtypeStruct((batch, columns), BF16),
+        ),
+        in_specs=[VMEM] * (len(parts) + 1),
+        out_specs=(VMEM, VMEM),
+        name="merge",
+    )(*parts, weight)
+
+
+def state_body(size, *refs):
+    parts, residual, gain, state_ref, out_ref = refs[:size], *refs[size:]
+    projected = pairwise([p[...].astype(F32) for p in parts], add)
+    state = (projected + residual[...].astype(F32)).astype(BF16)
+    state_ref[...] = state
+    state = state.astype(F32)
+    columns = state.shape[1]
+    out_ref[:, :columns] = (state * gain[...].astype(F32)).astype(BF16)
+    squares = jnp.sum(state * state, axis=1, keepdims=True)
+    lane = lax.broadcasted_iota(jnp.int32, (state.shape[0], LANES), 1)
+    value = jnp.zeros(lane.shape, F32)
+    for i, term in enumerate(split3(squares)):
+        value = jnp.where(lane == i, jnp.broadcast_to(term, lane.shape), value)
+    out_ref[:, columns:] = value.astype(BF16)
+
+
+def state(parts, residual, gain):
+    batch, columns = residual.shape
+    return pl.pallas_call(
+        functools.partial(state_body, len(parts)),
+        out_shape=(
+            jax.ShapeDtypeStruct((batch, columns), BF16),
+            jax.ShapeDtypeStruct((batch, columns + LANES), BF16),
+        ),
+        in_specs=[VMEM] * (len(parts) + 2),
+        out_specs=(VMEM, VMEM),
+        name="state",
+    )(*parts, residual, gain)
+
+
+def expert_body(size, *refs):
+    parts, (ids, probs, gate, up, down), outs = refs[:size], refs[size : size + 5], refs[size + 5 :]
+    columns = outs[0].shape[1]
+    me = lax.axis_index("kvp")
+    held = gate.shape[0]
+    squares = pairwise([jnp.sum(p[:, columns:].astype(F32), axis=1, keepdims=True) for p in parts], add)
+    inverse = lax.rsqrt(squares / (columns * size) + EPSILON)
+    sums = [0.0] * size
+    for e in range(held):
+        gate_sum, up_sum = 0.0, 0.0
+        for s in range(size):
+            rows = pl.ds(pl.multiple_of((me ^ s) * columns, LANES), columns)
+            block = parts[s][:, :columns]
+            gate_sum += jnp.dot(block, gate[e, rows, :], preferred_element_type=F32)
+            up_sum += jnp.dot(block, up[e, rows, :], preferred_element_type=F32)
+        gate_sum, up_sum = gate_sum * inverse, up_sum * inverse
+        hidden = (gate_sum / (1.0 + jnp.exp(-gate_sum)) * up_sum).astype(BF16)
+        chosen = ids[...] == me * held + e
+        scale = jnp.sum(jnp.where(chosen, probs[...], 0.0), axis=1, keepdims=True)
+        for s in range(size):
+            target = pl.ds(pl.multiple_of((me ^ s) * columns, LANES), columns)
+            sums[s] += jnp.dot(hidden, down[e, :, target], preferred_element_type=F32) * scale
+    for s in range(size):
+        outs[s][...] = sums[s].astype(BF16)
+
+
+def experts(parts, ids, probs, gate, up, down):
+    size = len(parts)
+    batch = parts[0].shape[0]
+    columns = parts[0].shape[1] - LANES
+    return pl.pallas_call(
+        functools.partial(expert_body, size),
+        out_shape=tuple(jax.ShapeDtypeStruct((batch, columns), BF16) for _ in range(size)),
+        in_specs=[VMEM] * (size + 5),
+        out_specs=(VMEM,) * size,
+        name="experts",
+    )(*parts, ids, probs, gate, up, down)
+
+
+def small_slice(
+    queries, keys, values, lengths, out_weight, residual, norm_gain, expert_ids, gate_probs, w_gate, w_up, w_down
+):
+    parts = exchange(attention(queries, keys, values, lengths), "kvp")
+    attended, projected = merge(parts, out_weight)
+    own_state, message = state(exchange(projected, "tp"), residual, norm_gain.reshape(1, -1))
+    outputs = experts(exchange(message, "kvp"), expert_ids, gate_probs, w_gate, w_up, w_down)
+    size = len(outputs)
+    moved = [outputs[0]] + [
+        lax.ppermute(outputs[s], "kvp", [(i, i ^ s) for i in range(size)]) for s in range(1, size)
+    ]
+    owned = pairwise([m.astype(F32) for m in moved], add).astype(BF16)
+    moe_term = pairwise([m.astype(F32) for m in exchange(owned, "tp")], add)
+    return attended, (own_state.astype(F32) + moe_term).astype(BF16)
 
 
 def merged(part, axis, combine):
@@ -51,7 +285,7 @@
     )
 
 
-def on_device(
+def large_slice(
     queries,
     keys,
     values,
@@ -104,7 +338,7 @@
     capacity = min(batch_size, max(2, 2 * batch_size * expert_ids.shape[1] // experts))
     dispatch, combine = slot_tables(expert_ids, gate_probs, experts, capacity)
     total_sq = lax.psum(jnp.sum(state_wide * state_wide, axis=1), "kvp")
-    inverse = lax.rsqrt(total_sq / D + EPSILON)
+    inverse = lax.rsqrt(total_sq / (col_count * shards) + EPSILON)
     normed = (state_wide * inverse[:, None] * norm_gain.astype(jnp.float32)[None, :]).astype(
         jnp.bfloat16
     )
@@ -126,6 +360,20 @@
     moe_term = lax.psum(moe_local, "tp")
     mixed = (state_wide + moe_term).astype(jnp.bfloat16)
     return (attended, mixed)
+
+
+def on_device(queries, keys, values, lengths, out_weight, *rest):
+    size, heads, kv = lax.axis_size("kvp"), queries.shape[1] // HEAD, keys.shape[2] // HEAD
+    direct = (
+        size in (2, 4, 8)
+        and lax.axis_size("tp") in (2, 4, 8)
+        and out_weight.shape[1] % LANES == 0
+        and kv == 2
+        and heads == 8 * kv
+        and keys.shape[1] % LANES == 0
+        and queries.shape[0] == 16
+    )
+    return (small_slice if direct else large_slice)(queries, keys, values, lengths, out_weight, *rest)
 
 
 def solution(mesh):

time: 126 us -> 53.4 us (0.42)
  blocking collectives: 93.8 us -> 0 us
  starting transfers between devices: 0 us -> 17.8 us
  waiting for transfers between devices: 0 us -> 15.3 us
  Pallas kernels: 0 us -> 14.2 us
  other arithmetic: 15.3 us -> 1.33 us
  matrix products: 6.53 us -> 0 us
  local copies, waits for them, and re-layouts: 8.31 us -> 3.77 us
    all_gather x3 -> x0, blocking collectives: 43.4 us -> none  [merged(): gathered = jax.tree.map(lambda a: lax.all_gather(a, axis), part)]
    psum x3 -> x0, blocking collectives: 34.1 us -> none  [the longest x1 12.5 us: on_device(): total_sq = lax.psum(jnp.sum(state_wide * state_wide, axis=1), 'kvp')]
    ppermute x0 -> x15, starting transfers between devices: none -> 17.8 us  [the longest x12 13.9 us: exchange(): lax.ppermute(x, axis, [(i, i ^ s) for i in range(size)])]
    all_to_all x2 -> x0, blocking collectives: 16.3 us -> none  [the longest x1 8.21 us: on_device(): lax.all_to_all(partial_value, 'kvp', split_axis=2, concat_axis=0, tiled=T...]
    ppermute x0 -> x15, waiting for transfers between devices: none -> 15.3 us  [the longest x12 12 us: exchange(): lax.ppermute(x, axis, [(i, i ^ s) for i in range(size)])]
    pallas_call x0 -> x4, Pallas kernels: none -> 14.2 us  [the longest x1 6.95 us: attention(): pl.pallas_call(functools.partial(attention_body, heads, width // HEAD, ch...]
    unnamed x1 -> x0, other arithmetic: 7.21 us -> none
    dot_general x7 -> x0, matrix products: 6.53 us -> none  [the longest x1 2.07 us: on_device(): jnp.dot(attended.astype(jnp.bfloat16), out_weight, preferred_element_type...]
  transfers between devices with their start and end apart: 0 -> 15, of which waited for: 0 -> 10; matrix products, arithmetic and copies ran while one was open for 0% -> 4% of each run, Pallas kernels for 0% -> 0%
where the time goes in v1:
time: 53.4 us; the launch traced here: 53.1 us
  starting transfers between devices  17.8 us (33%)
  waiting for transfers between devices  15.3 us (29%)
  Pallas kernels  14.2 us (27%)
  local copies, waits for them, and re-layouts  3.77 us (7%)
  other arithmetic  1.33 us (2%)
  between operations  0.72 us (1%)
    ppermute x12, starting transfers between devices, exchange(): lax.ppermute(x, axis, [(i, i ^ s) for i in range(size)])  13.9 us
    ppermute x12, waiting for transfers between devices, exchange(): lax.ppermute(x, axis, [(i, i ^ s) for i in range(size)])  12 us
    pallas_call x1, Pallas kernels, attention(): pl.pallas_call(functools.partial(attention_body, heads, width // HEAD, ch...  6.95 us
    ppermute x3, starting transfers between devices, small_slice(): lax.ppermute(outputs[s], 'kvp', [(i, i ^ s) for i in range(size)])  3.9 us
    pallas_call x1, Pallas kernels, experts(): pl.pallas_call(functools.partial(expert_body, size), out_shape=tuple((jax...  3.41 us
    ppermute x3, waiting for transfers between devices, small_slice(): lax.ppermute(outputs[s], 'kvp', [(i, i ^ s) for i in range(size)])  3.37 us
    unnamed x28, local copies, waits for them, and re-layouts  3.18 us
    pallas_call x1, Pallas kernels, merge(): pl.pallas_call(functools.partial(merge_body, inputs // HEAD, len(parts)),...  2.32 us
  transfers between devices with their start and end apart: 15, of which 10 were waited for; matrix products, arithmetic and copies ran while one was open for 4% of the time, Pallas kernels for 0%

profile of v1, /device:TPU:0, one launch (start us, length us, event | category | flops | bytes accessed | tf_op | source)
XLA Modules:
  0.0 53.1 jit_solution(6786194287669205709)
XLA Ops:
  0.6 0.0 copy-start.12
  0.6 0.0 copy-start.10
  0.7 7.0 %attention.1.refs_0_ = bf16[16,1152]{1,0:T(8,128)(2,1)} custom-call(s32[16]{0:T(128)} %len_ref.1, bf16[16,1024]{1,0:T(8,128)(2,1)} %q_ref.1, bf16[16,128,128]{2,1,0:T(8,128)(2,1)} %k_hbm.1, bf16[16,128,128]{2,1,0:T(8,128)(2,1)} %v_hbm.1), custom_call_target="tpu_custom_call" | custom-call | tf_op jit(solution)/shard_map/attention/pallas_call | solution.py:103
  7.6 3.1 %collective-permute-start = (bf16[16,1152]{1,0:T(8,128)(2,1)}, bf16[16,1152]{1,0:T(8,128)(2,1)S(1)}, u32[]{:S(2)}, u32[]{:S(2)}) collective-permute-start(bf16[16,1152]{1,0:T(8,128)(2,1)} %attention.1.refs_0_), channel_id=1, source_target_pairs={{0,4},{4,0},{8,12},{12,8},{1,5},{5,1},{9,13},{13,9},{2,6},{6,2},{1... | collective-permute-start | bytes 110600 | tf_op jit(solution)/shard_map/ppermute | solution.py:23
  10.7 2.6 %collective-permute-start.1 = (bf16[16,1152]{1,0:T(8,128)(2,1)}, bf16[16,1152]{1,0:T(8,128)(2,1)S(1)}, u32[]{:S(2)}, u32[]{:S(2)}) collective-permute-start(bf16[16,1152]{1,0:T(8,128)(2,1)} %attention.1.refs_0_), channel_id=1, source_target_pairs={{0,8},{4,12},{8,0},{12,4},{1,9},{5,13},{9,1},{13,5},{2,10},{6,14},... | collective-permute-start | bytes 110600 | tf_op jit(solution)/shard_map/ppermute | solution.py:23
  13.3 0.0 collective-permute-start.2
  13.3 0.0 collective-permute-done.refs_1_
  13.3 3.1 %collective-permute-done.1.refs_2_ = bf16[16,1152]{1,0:T(8,128)(2,1)S(1)} collective-permute-done((bf16[16,1152]{1,0:T(8,128)(2,1)}, bf16[16,1152]{1,0:T(8,128)(2,1)S(1)}, u32[]{:S(2)}, u32[]{:S(2)}) %collective-permute-start.1) | collective-permute-done | bytes 36896 | tf_op jit(solution)/shard_map/ppermute | solution.py:23
  16.5 2.8 %collective-permute-done.2.refs_3_ = bf16[16,1152]{1,0:T(8,128)(2,1)S(1)} collective-permute-done((bf16[16,1152]{1,0:T(8,128)(2,1)}, bf16[16,1152]{1,0:T(8,128)(2,1)S(1)}, u32[]{:S(2)}, u32[]{:S(2)}) %collective-permute-start.2) | collective-permute-done | bytes 36896 | tf_op jit(solution)/shard_map/ppermute | solution.py:23
  19.3 0.0 copy-done
  19.3 0.6 %copy-done.2 = bf16[16,1152]{1,0:T(8,128)(2,1)} copy-done((bf16[16,1152]{1,0:T(8,128)(2,1)}, bf16[16,1152]{1,0:T(8,128)(2,1)S(1)}, u32[]{:S(2)}) %copy-start.2) | copy-done | bytes 36888
  19.9 2.3 %merge.1 = (f32[16,1024]{1,0:T(8,128)}, bf16[16,384]{1,0:T(8,128)(2,1)}) custom-call(bf16[16,1152]{1,0:T(8,128)(2,1)} %attention.1.refs_0_, bf16[16,1152]{1,0:T(8,128)(2,1)} %copy-done, bf16[16,1152]{1,0:T(8,128)(2,1)} %copy-done.1, bf16[16,1152]{1,0:T(8,128)(2,1)} %copy-done.2, bf16[1024,384]{1,0:T(8,128)(2,1)} %refs_4_.3), custom_call_target="tpu_custom_call" | custom-call | tf_op jit(solution)/shard_map/merge/pallas_call | solution.py:151
  22.2 0.0 collective-permute-start.3
  22.2 1.5 %collective-permute-start.4 = (bf16[16,384]{1,0:T(8,128)(2,1)}, bf16[16,384]{1,0:T(8,128)(2,1)S(1)}, u32[]{:S(2)}, u32[]{:S(2)}) collective-permute-start(bf16[16,384]{1,0:T(8,128)(2,1)} %get-tuple-element.11.refs_0_), channel_id=1, source_target_pairs={{0,2},{1,3},{2,0},{3,1},{4,6},{5,7},{6,4},{7,5},{8,10},{9,11},{10,... | collective-permute-start | bytes 36872 | tf_op jit(solution)/shard_map/ppermute | solution.py:23
  23.7 0.4 collective-permute-start.5
  24.1 0.6 %reshape.7.refs_5_ = bf16[1,384]{1,0:T(2,128)(2,1)} reshape(bf16[384]{0:T(512)(128)(2,1)S(1)} %copy-done.12) | data formatting | bytes 1536 | tf_op jit(solution)/shard_map/reshape | solution.py:237
  24.7 0.0 collective-permute-done.3.refs_1_
  24.7 1.4 %collective-permute-done.4.refs_2_ = bf16[16,384]{1,0:T(8,128)(2,1)S(1)} collective-permute-done((bf16[16,384]{1,0:T(8,128)(2,1)}, bf16[16,384]{1,0:T(8,128)(2,1)S(1)}, u32[]{:S(2)}, u32[]{:S(2)}) %collective-permute-start.4) | collective-permute-done | bytes 12320 | tf_op jit(solution)/shard_map/ppermute | solution.py:23
  26.1 0.9 %collective-permute-done.5.refs_3_ = bf16[16,384]{1,0:T(8,128)(2,1)S(1)} collective-permute-done((bf16[16,384]{1,0:T(8,128)(2,1)}, bf16[16,384]{1,0:T(8,128)(2,1)S(1)}, u32[]{:S(2)}, u32[]{:S(2)}) %collective-permute-start.5) | collective-permute-done | bytes 12320 | tf_op jit(solution)/shard_map/ppermute | solution.py:23
  27.1 0.6 %copy-done.9 = bf16[16,384]{1,0:T(8,128)(2,1)} copy-done((bf16[16,384]{1,0:T(8,128)(2,1)}, bf16[16,384]{1,0:T(8,128)(2,1)S(1)}, u32[]{:S(2)}) %copy-start.9) | copy-done | bytes 12312
  27.7 1.5 %state.1 = (bf16[16,384]{1,0:T(8,128)(2,1)}, bf16[16,512]{1,0:T(8,128)(2,1)}) custom-call(bf16[16,384]{1,0:T(8,128)(2,1)} %get-tuple-element.11.refs_0_, bf16[16,384]{1,0:T(8,128)(2,1)} %copy-done.7, bf16[16,384]{1,0:T(8,128)(2,1)} %copy-done.8, bf16[16,384]{1,0:T(8,128)(2,1)} %copy-done.9, bf16[16,384]{1,0:T(8,128)(2,1)} %refs_4_.4, ...), custom_call_target="tpu_custom_call" | custom-call | tf_op jit(solution)/shard_map/state/pallas_call | solution.py:181
  29.1 0.0 collective-permute-start.6
  29.1 1.1 %collective-permute-start.7 = (bf16[16,512]{1,0:T(8,128)(2,1)}, bf16[16,512]{1,0:T(8,128)(2,1)S(1)}, u32[]{:S(2)}, u32[]{:S(2)}) collective-permute-start(bf16[16,512]{1,0:T(8,128)(2,1)} %get-tuple-element.13.refs_0_), channel_id=1, source_target_pairs={{0,8},{4,12},{8,0},{12,4},{1,9},{5,13},{9,1},{13,5},{2,10},{6,14},... | collective-permute-start | bytes 49160 | tf_op jit(solution)/shard_map/ppermute | solution.py:23
  30.2 3.3 %collective-permute-start.8 = (bf16[16,512]{1,0:T(8,128)(2,1)}, bf16[16,512]{1,0:T(8,128)(2,1)S(1)}, u32[]{:S(2)}, u32[]{:S(2)}) collective-permute-start(bf16[16,512]{1,0:T(8,128)(2,1)} %get-tuple-element.13.refs_0_), channel_id=1, source_target_pairs={{0,12},{4,8},{8,4},{12,0},{1,13},{5,9},{9,5},{13,1},{2,14},{6,10},... | collective-permute-start | bytes 49160 | tf_op jit(solution)/shard_map/ppermute | solution.py:23
  33.5 0.0 copy-done.10
  33.5 0.7 %copy.14.refs_4_ = s32[16,4]{1,0:T(8,128)} copy(s32[16,4]{0,1:T(4,128)S(1)} %copy-done.10) | data formatting | bytes 512 | tf_op args[7]
  34.2 0.7 %copy.15.refs_5_ = f32[16,4]{1,0:T(8,128)} copy(f32[16,4]{0,1:T(4,128)S(1)} %copy-done.11) | data formatting | bytes 512 | tf_op args[8]
  34.9 0.0 collective-permute-done.6.refs_1_
  34.9 0.0 collective-permute-done.7.refs_2_
  34.9 0.0 copy-start.4
  34.9 1.1 %collective-permute-done.8.refs_3_ = bf16[16,512]{1,0:T(8,128)(2,1)S(1)} collective-permute-done((bf16[16,512]{1,0:T(8,128)(2,1)}, bf16[16,512]{1,0:T(8,128)(2,1)S(1)}, u32[]{:S(2)}, u32[]{:S(2)}) %collective-permute-start.8) | collective-permute-done | bytes 16416 | tf_op jit(solution)/shard_map/ppermute | solution.py:23
  35.9 0.0 copy-done.4
  35.9 0.6 %copy-done.5 = bf16[16,512]{1,0:T(8,128)(2,1)} copy-done((bf16[16,512]{1,0:T(8,128)(2,1)}, bf16[16,512]{1,0:T(8,128)(2,1)S(1)}, u32[]{:S(2)}) %copy-start.5) | copy-done | bytes 16408
  36.6 3.4 %experts.1 = (bf16[16,384]{1,0:T(8,128)(2,1)}, bf16[16,384]{1,0:T(8,128)(2,1)}, bf16[16,384]{1,0:T(8,128)(2,1)}, bf16[16,384]{1,0:T(8,128)(2,1)}) custom-call(bf16[16,512]{1,0:T(8,128)(2,1)} %get-tuple-element.13.refs_0_, bf16[16,512]{1,0:T(8,128)(2,1)} %copy-done.3, bf16[16,512]{1,0:T(8,128)(2,1)} %copy-done.4, bf16[16,512]{1,0:T(8,128)(2,1)} %copy-done.5, ...), custom_call_target="tpu_custom_call" | custom-call | tf_op jit(solution)/shard_map/experts/pallas_call | solution.py:223
  40.0 0.1 collective-permute-start.10
  40.0 3.3 %collective-permute-start.11 = (bf16[16,384]{1,0:T(8,128)(2,1)}, bf16[16,384]{1,0:T(8,128)(2,1)S(1)}, u32[]{:S(2)}, u32[]{:S(2)}) collective-permute-start(bf16[16,384]{1,0:T(8,128)(2,1)} %get-tuple-element.17), channel_id=1, source_target_pairs={{0,12},{4,8},{8,4},{12,0},{1,13},{5,9},{9,5},{13,1},{2,14},{6,10},... | collective-permute-start | bytes 36872 | tf_op jit(solution)/shard_map/ppermute | solution.py:241
  43.3 0.5 %collective-permute-start.9 = (bf16[16,384]{1,0:T(8,128)(2,1)}, bf16[16,384]{1,0:T(8,128)(2,1)S(1)}, u32[]{:S(2)}, u32[]{:S(2)}) collective-permute-start(bf16[16,384]{1,0:T(8,128)(2,1)} %get-tuple-element.15), channel_id=1, source_target_pairs={{0,4},{4,0},{8,12},{12,8},{1,5},{5,1},{9,13},{13,9},{2,6},{6,2},{1... | collective-permute-start | bytes 36872 | tf_op jit(solution)/shard_map/ppermute | solution.py:241
  43.9 0.9 %collective-permute-done.10 = bf16[16,384]{1,0:T(8,128)(2,1)S(1)} collective-permute-done((bf16[16,384]{1,0:T(8,128)(2,1)}, bf16[16,384]{1,0:T(8,128)(2,1)S(1)}, u32[]{:S(2)}, u32[]{:S(2)}) %collective-permute-start.10) | collective-permute-done | bytes 12320 | tf_op jit(solution)/shard_map/ppermute | solution.py:241
  44.8 1.0 %collective-permute-done.11 = bf16[16,384]{1,0:T(8,128)(2,1)S(1)} collective-permute-done((bf16[16,384]{1,0:T(8,128)(2,1)}, bf16[16,384]{1,0:T(8,128)(2,1)S(1)}, u32[]{:S(2)}, u32[]{:S(2)}) %collective-permute-start.11) | collective-permute-done | bytes 12320 | tf_op jit(solution)/shard_map/ppermute | solution.py:241
  45.8 1.5 %collective-permute-done.9 = bf16[16,384]{1,0:T(8,128)(2,1)S(1)} collective-permute-done((bf16[16,384]{1,0:T(8,128)(2,1)}, bf16[16,384]{1,0:T(8,128)(2,1)S(1)}, u32[]{:S(2)}, u32[]{:S(2)}) %collective-permute-start.9) | collective-permute-done | bytes 12320 | tf_op jit(solution)/shard_map/ppermute | solution.py:241
  47.2 0.7 %add_convert_fusion.1 = bf16[16,384]{1,0:T(8,128)(2,1)S(1)} fusion(bf16[16,384]{1,0:T(8,128)(2,1)S(1)} %collective-permute-done.11, bf16[16,384]{1,0:T(8,128)(2,1)S(1)} %collective-permute-done.10, bf16[16,384]{1,0:T(8,128)(2,1)S(1)} %collective-permute-done.9, bf16[16,384]{1,0:T(8,128)(2,1)} %get-tuple-element.14), kind=kLoop, calls=%fused_computation.1 | loop fusion | flops 49152 | bytes 61440 | tf_op jit(solution)/shard_map/convert_element_type | solution.py:243
  48.0 0.1 collective-permute-start.12
  48.0 1.3 %collective-permute-start.13 = (bf16[16,384]{1,0:T(8,128)(2,1)S(1)}, bf16[16,384]{1,0:T(8,128)(2,1)S(1)}, u32[]{:S(2)}, u32[]{:S(2)}) collective-permute-start(bf16[16,384]{1,0:T(8,128)(2,1)S(1)} %add_convert_fusion.1), channel_id=1, source_target_pairs={{0,2},{1,3},{2,0},{3,1},{4,6},{5,7},{6,4},{7,5},{8,10},{9,11},{10,... | collective-permute-start | bytes 36872 | tf_op jit(solution)/shard_map/ppermute | solution.py:23
  49.4 0.5 collective-permute-start.14
  49.9 0.0 collective-permute-done.12
  49.9 1.9 %collective-permute-done.13 = bf16[16,384]{1,0:T(8,128)(2,1)S(1)} collective-permute-done((bf16[16,384]{1,0:T(8,128)(2,1)S(1)}, bf16[16,384]{1,0:T(8,128)(2,1)S(1)}, u32[]{:S(2)}, u32[]{:S(2)}) %collective-permute-start.13) | collective-permute-done | bytes 12320 | tf_op jit(solution)/shard_map/ppermute | solution.py:23
  51.8 0.7 %collective-permute-done.14 = bf16[16,384]{1,0:T(8,128)(2,1)S(1)} collective-permute-done((bf16[16,384]{1,0:T(8,128)(2,1)S(1)}, bf16[16,384]{1,0:T(8,128)(2,1)S(1)}, u32[]{:S(2)}, u32[]{:S(2)}) %collective-permute-start.14) | collective-permute-done | bytes 12320 | tf_op jit(solution)/shard_map/ppermute | solution.py:23
  52.5 0.6 %add_convert_fusion = bf16[16,384]{1,0:T(8,128)(2,1)} fusion(bf16[16,384]{1,0:T(8,128)(2,1)S(1)} %collective-permute-done.14, bf16[16,384]{1,0:T(8,128)(2,1)S(1)} %collective-permute-done.13, bf16[16,384]{1,0:T(8,128)(2,1)S(1)} %collective-permute-done.12, bf16[16,384]{1,0:T(8,128)(2,1)S(1)} %add_convert_fusion.1, bf16[16,384]{1,0:T(8,128)(2,1)S(1)} %copy-done.6), kind=kLoop, calls=%fused_computation | loop fusion | flops 61440 | bytes 73728 | tf_op jit(solution)/shard_map/convert_element_type | solution.py:245
  (17 shorter events, 0.0 us)
Async XLA Ops:
  0.6 23.5 %copy-start.12 = (bf16[384]{0:T(512)(128)(2,1)S(1)}, bf16[384]{0:T(512)(128)(2,1)}, u32[]{:S(2)}) copy-start(bf16[384]{0:T(512)(128)(2,1)} %param.18) | copy-start | bytes 2308
  0.6 32.9 %copy-start.10 = (s32[16,4]{0,1:T(4,128)S(1)}, s32[16,4]{0,1:T(4,128)}, u32[]{:S(2)}) copy-start(s32[16,4]{0,1:T(4,128)} %param.19) | copy-start | bytes 772
  0.7 33.6 %copy-start.11 = (f32[16,4]{0,1:T(4,128)S(1)}, f32[16,4]{0,1:T(4,128)}, u32[]{:S(2)}) copy-start(f32[16,4]{0,1:T(4,128)} %param.20) | copy-start | bytes 772
  7.6 5.7 %collective-permute-start = (bf16[16,1152]{1,0:T(8,128)(2,1)}, bf16[16,1152]{1,0:T(8,128)(2,1)S(1)}, u32[]{:S(2)}, u32[]{:S(2)}) collective-permute-start(bf16[16,1152]{1,0:T(8,128)(2,1)} %attention.1.refs_0_), channel_id=1, source_target_pairs={{0,4},{4,0},{8,12},{12,8},{1,5},{5,1},{9,13},{13,9},{2,6},{6,2},{1... | collective-permute-start | bytes 110600 | tf_op jit(solution)/shard_map/ppermute | solution.py:23
  10.7 5.7 %collective-permute-start.1 = (bf16[16,1152]{1,0:T(8,128)(2,1)}, bf16[16,1152]{1,0:T(8,128)(2,1)S(1)}, u32[]{:S(2)}, u32[]{:S(2)}) collective-permute-start(bf16[16,1152]{1,0:T(8,128)(2,1)} %attention.1.refs_0_), channel_id=1, source_target_pairs={{0,8},{4,12},{8,0},{12,4},{1,9},{5,13},{9,1},{13,5},{2,10},{6,14},... | collective-permute-start | bytes 110600 | tf_op jit(solution)/shard_map/ppermute | solution.py:23
  13.3 6.0 %collective-permute-start.2 = (bf16[16,1152]{1,0:T(8,128)(2,1)}, bf16[16,1152]{1,0:T(8,128)(2,1)S(1)}, u32[]{:S(2)}, u32[]{:S(2)}) collective-permute-start(bf16[16,1152]{1,0:T(8,128)(2,1)} %attention.1.refs_0_), channel_id=1, source_target_pairs={{0,12},{4,8},{8,4},{12,0},{1,13},{5,9},{9,5},{13,1},{2,14},{6,10},... | collective-permute-start | bytes 110600 | tf_op jit(solution)/shard_map/ppermute | solution.py:23
  13.3 6.0 %copy-start = (bf16[16,1152]{1,0:T(8,128)(2,1)}, bf16[16,1152]{1,0:T(8,128)(2,1)S(1)}, u32[]{:S(2)}) copy-start(bf16[16,1152]{1,0:T(8,128)(2,1)S(1)} %collective-permute-done.refs_1_) | copy-start | bytes 110596
  16.5 2.8 %copy-start.1 = (bf16[16,1152]{1,0:T(8,128)(2,1)}, bf16[16,1152]{1,0:T(8,128)(2,1)S(1)}, u32[]{:S(2)}) copy-start(bf16[16,1152]{1,0:T(8,128)(2,1)S(1)} %collective-permute-done.1.refs_2_) | copy-start | bytes 110596
  19.3 0.6 %copy-start.2 = (bf16[16,1152]{1,0:T(8,128)(2,1)}, bf16[16,1152]{1,0:T(8,128)(2,1)S(1)}, u32[]{:S(2)}) copy-start(bf16[16,1152]{1,0:T(8,128)(2,1)S(1)} %collective-permute-done.2.refs_3_) | copy-start | bytes 110596
  22.2 2.5 %collective-permute-start.3 = (bf16[16,384]{1,0:T(8,128)(2,1)}, bf16[16,384]{1,0:T(8,128)(2,1)S(1)}, u32[]{:S(2)}, u32[]{:S(2)}) collective-permute-start(bf16[16,384]{1,0:T(8,128)(2,1)} %get-tuple-element.11.refs_0_), channel_id=1, source_target_pairs={{0,1},{1,0},{2,3},{3,2},{4,5},{5,4},{6,7},{7,6},{8,9},{9,8},{10,11... | collective-permute-start | bytes 36872 | tf_op jit(solution)/shard_map/ppermute | solution.py:23
  22.2 3.9 %collective-permute-start.4 = (bf16[16,384]{1,0:T(8,128)(2,1)}, bf16[16,384]{1,0:T(8,128)(2,1)S(1)}, u32[]{:S(2)}, u32[]{:S(2)}) collective-permute-start(bf16[16,384]{1,0:T(8,128)(2,1)} %get-tuple-element.11.refs_0_), channel_id=1, source_target_pairs={{0,2},{1,3},{2,0},{3,1},{4,6},{5,7},{6,4},{7,5},{8,10},{9,11},{10,... | collective-permute-start | bytes 36872 | tf_op jit(solution)/shard_map/ppermute | solution.py:23
  23.7 3.3 %collective-permute-start.5 = (bf16[16,384]{1,0:T(8,128)(2,1)}, bf16[16,384]{1,0:T(8,128)(2,1)S(1)}, u32[]{:S(2)}, u32[]{:S(2)}) collective-permute-start(bf16[16,384]{1,0:T(8,128)(2,1)} %get-tuple-element.11.refs_0_), channel_id=1, source_target_pairs={{0,3},{1,2},{2,1},{3,0},{4,7},{5,6},{6,5},{7,4},{8,11},{9,10},{10,... | collective-permute-start | bytes 36872 | tf_op jit(solution)/shard_map/ppermute | solution.py:23
  24.7 2.4 %copy-start.7 = (bf16[16,384]{1,0:T(8,128)(2,1)}, bf16[16,384]{1,0:T(8,128)(2,1)S(1)}, u32[]{:S(2)}) copy-start(bf16[16,384]{1,0:T(8,128)(2,1)S(1)} %collective-permute-done.3.refs_1_) | copy-start | bytes 36868
  26.1 0.9 %copy-start.8 = (bf16[16,384]{1,0:T(8,128)(2,1)}, bf16[16,384]{1,0:T(8,128)(2,1)S(1)}, u32[]{:S(2)}) copy-start(bf16[16,384]{1,0:T(8,128)(2,1)S(1)} %collective-permute-done.4.refs_2_) | copy-start | bytes 36868
  27.1 0.6 %copy-start.9 = (bf16[16,384]{1,0:T(8,128)(2,1)}, bf16[16,384]{1,0:T(8,128)(2,1)S(1)}, u32[]{:S(2)}) copy-start(bf16[16,384]{1,0:T(8,128)(2,1)S(1)} %collective-permute-done.5.refs_3_) | copy-start | bytes 36868
  29.1 5.7 %collective-permute-start.6 = (bf16[16,512]{1,0:T(8,128)(2,1)}, bf16[16,512]{1,0:T(8,128)(2,1)S(1)}, u32[]{:S(2)}, u32[]{:S(2)}) collective-permute-start(bf16[16,512]{1,0:T(8,128)(2,1)} %get-tuple-element.13.refs_0_), channel_id=1, source_target_pairs={{0,4},{4,0},{8,12},{12,8},{1,5},{5,1},{9,13},{13,9},{2,6},{6,2},{1... | collective-permute-start | bytes 49160 | tf_op jit(solution)/shard_map/ppermute | solution.py:23
  29.1 5.7 %collective-permute-start.7 = (bf16[16,512]{1,0:T(8,128)(2,1)}, bf16[16,512]{1,0:T(8,128)(2,1)S(1)}, u32[]{:S(2)}, u32[]{:S(2)}) collective-permute-start(bf16[16,512]{1,0:T(8,128)(2,1)} %get-tuple-element.13.refs_0_), channel_id=1, source_target_pairs={{0,8},{4,12},{8,0},{12,4},{1,9},{5,13},{9,1},{13,5},{2,10},{6,14},... | collective-permute-start | bytes 49160 | tf_op jit(solution)/shard_map/ppermute | solution.py:23
  30.2 5.7 %collective-permute-start.8 = (bf16[16,512]{1,0:T(8,128)(2,1)}, bf16[16,512]{1,0:T(8,128)(2,1)S(1)}, u32[]{:S(2)}, u32[]{:S(2)}) collective-permute-start(bf16[16,512]{1,0:T(8,128)(2,1)} %get-tuple-element.13.refs_0_), channel_id=1, source_target_pairs={{0,12},{4,8},{8,4},{12,0},{1,13},{5,9},{9,5},{13,1},{2,14},{6,10},... | collective-permute-start | bytes 49160 | tf_op jit(solution)/shard_map/ppermute | solution.py:23
  34.9 17.6 %copy-start.6 = (bf16[16,384]{1,0:T(8,128)(2,1)S(1)}, bf16[16,384]{1,0:T(8,128)(2,1)}, u32[]{:S(2)}) copy-start(bf16[16,384]{1,0:T(8,128)(2,1)} %get-tuple-element.12) | copy-start | bytes 36868
  34.9 1.1 %copy-start.3 = (bf16[16,512]{1,0:T(8,128)(2,1)}, bf16[16,512]{1,0:T(8,128)(2,1)S(1)}, u32[]{:S(2)}) copy-start(bf16[16,512]{1,0:T(8,128)(2,1)S(1)} %collective-permute-done.6.refs_1_) | copy-start | bytes 49156
  34.9 1.1 %copy-start.4 = (bf16[16,512]{1,0:T(8,128)(2,1)}, bf16[16,512]{1,0:T(8,128)(2,1)S(1)}, u32[]{:S(2)}) copy-start(bf16[16,512]{1,0:T(8,128)(2,1)S(1)} %collective-permute-done.7.refs_2_) | copy-start | bytes 49156
  35.9 0.6 %copy-start.5 = (bf16[16,512]{1,0:T(8,128)(2,1)}, bf16[16,512]{1,0:T(8,128)(2,1)S(1)}, u32[]{:S(2)}) copy-start(bf16[16,512]{1,0:T(8,128)(2,1)S(1)} %collective-permute-done.8.refs_3_) | copy-start | bytes 49156
  40.0 4.8 %collective-permute-start.10 = (bf16[16,384]{1,0:T(8,128)(2,1)}, bf16[16,384]{1,0:T(8,128)(2,1)S(1)}, u32[]{:S(2)}, u32[]{:S(2)}) collective-permute-start(bf16[16,384]{1,0:T(8,128)(2,1)} %get-tuple-element.16), channel_id=1, source_target_pairs={{0,8},{4,12},{8,0},{12,4},{1,9},{5,13},{9,1},{13,5},{2,10},{6,14},... | collective-permute-start | bytes 36872 | tf_op jit(solution)/shard_map/ppermute | solution.py:241
  40.0 5.7 %collective-permute-start.11 = (bf16[16,384]{1,0:T(8,128)(2,1)}, bf16[16,384]{1,0:T(8,128)(2,1)S(1)}, u32[]{:S(2)}, u32[]{:S(2)}) collective-permute-start(bf16[16,384]{1,0:T(8,128)(2,1)} %get-tuple-element.17), channel_id=1, source_target_pairs={{0,12},{4,8},{8,4},{12,0},{1,13},{5,9},{9,5},{13,1},{2,14},{6,10},... | collective-permute-start | bytes 36872 | tf_op jit(solution)/shard_map/ppermute | solution.py:241
  43.3 3.9 %collective-permute-start.9 = (bf16[16,384]{1,0:T(8,128)(2,1)}, bf16[16,384]{1,0:T(8,128)(2,1)S(1)}, u32[]{:S(2)}, u32[]{:S(2)}) collective-permute-start(bf16[16,384]{1,0:T(8,128)(2,1)} %get-tuple-element.15), channel_id=1, source_target_pairs={{0,4},{4,0},{8,12},{12,8},{1,5},{5,1},{9,13},{13,9},{2,6},{6,2},{1... | collective-permute-start | bytes 36872 | tf_op jit(solution)/shard_map/ppermute | solution.py:241
  48.0 1.9 %collective-permute-start.12 = (bf16[16,384]{1,0:T(8,128)(2,1)S(1)}, bf16[16,384]{1,0:T(8,128)(2,1)S(1)}, u32[]{:S(2)}, u32[]{:S(2)}) collective-permute-start(bf16[16,384]{1,0:T(8,128)(2,1)S(1)} %add_convert_fusion.1), channel_id=1, source_target_pairs={{0,1},{1,0},{2,3},{3,2},{4,5},{5,4},{6,7},{7,6},{8,9},{9,8},{10,11... | collective-permute-start | bytes 36872 | tf_op jit(solution)/shard_map/ppermute | solution.py:23
  48.0 3.8 %collective-permute-start.13 = (bf16[16,384]{1,0:T(8,128)(2,1)S(1)}, bf16[16,384]{1,0:T(8,128)(2,1)S(1)}, u32[]{:S(2)}, u32[]{:S(2)}) collective-permute-start(bf16[16,384]{1,0:T(8,128)(2,1)S(1)} %add_convert_fusion.1), channel_id=1, source_target_pairs={{0,2},{1,3},{2,0},{3,1},{4,6},{5,7},{6,4},{7,5},{8,10},{9,11},{10,... | collective-permute-start | bytes 36872 | tf_op jit(solution)/shard_map/ppermute | solution.py:23
  49.4 3.1 %collective-permute-start.14 = (bf16[16,384]{1,0:T(8,128)(2,1)S(1)}, bf16[16,384]{1,0:T(8,128)(2,1)S(1)}, u32[]{:S(2)}, u32[]{:S(2)}) collective-permute-start(bf16[16,384]{1,0:T(8,128)(2,1)S(1)} %add_convert_fusion.1), channel_id=1, source_target_pairs={{0,3},{1,2},{2,1},{3,0},{4,7},{5,6},{6,5},{7,4},{8,11},{9,10},{10,... | collective-permute-start | bytes 36872 | tf_op jit(solution)/shard_map/ppermute | solution.py:23

commit v2 on v1

--- a/solution.py
+++ b/solution.py
@@ -7,21 +7,37 @@
 from jax.experimental.pallas import tpu as pltpu
 from jax.sharding import PartitionSpec as P
 
+
 HEAD = 64
 LANES = 128
 EPSILON = 1e-05
 NEGATIVE = -1e30
 F32 = jnp.float32
 BF16 = jnp.bfloat16
+LIMIT = pltpu.CompilerParams(vmem_limit_bytes=8 * 1024 * 1024)
 VMEM = pl.BlockSpec(memory_space=pltpu.VMEM)
-SMEM = pl.BlockSpec(memory_space=pltpu.SMEM)
-ANY = pl.BlockSpec(memory_space=pl.ANY)
-
-
-def exchange(x, axis):
-    size = lax.axis_size(axis)
-    moved = [lax.ppermute(x, axis, [(i, i ^ s) for i in range(size)]) for s in range(size - 1, 0, -1)]
-    return [x] + moved[::-1]
+HBM = pl.BlockSpec(memory_space=pltpu.HBM)
+
+
+def turn(x, axis, s):
+    return lax.ppermute(x, axis, [(i, i ^ s) for i in range(lax.axis_size(axis))])
+
+
+def exchange(blocks, axis):
+    moved = {s: turn(blocks[s], axis, s) for s in range(len(blocks) - 1, 0, -1)}
+    return [blocks[0]] + [moved[s] for s in range(1, len(blocks))]
+
+
+def share(x, axis):
+    return exchange([x] * lax.axis_size(axis), axis)
+
+
+def on_chip(x):
+    return pltpu.with_memory_space_constraint(x, pltpu.VMEM)
+
+
+def off_chip(x):
+    return pltpu.with_memory_space_constraint(x, pltpu.HBM)
 
 
 def pairwise(parts, add):
@@ -42,78 +58,91 @@
     return first, second, (rest - second).astype(BF16).astype(F32)
 
 
-def attention_body(heads, kv, chunks, len_ref, q_ref, k_hbm, v_hbm, out_ref, k_buf, v_buf, rows, stats, sems):
+def attention_body(heads, kv, held, *refs):
+    len_hbm, q_hbm, k_hbm, v_hbm = refs[:4]
+    sources, out_ref, targets = refs[4 : 4 + held], refs[4 + held], refs[5 + held : 5 + 2 * held]
+    lengths, q_buf, k_buf, v_buf, rows, sems = refs[5 + 2 * held :]
     batch, context = k_buf.shape[:2]
     group = heads // kv
-    step = batch // chunks
-
-    def copy(source, target, which, c):
-        part = pl.ds(c * step, step)
-        return pltpu.make_async_copy(source.at[part], target.at[part], sems.at[which, c])
-
-    for c in range(chunks):
-        copy(k_hbm, k_buf, 0, c).start()
-    for c in range(chunks):
-        copy(v_hbm, v_buf, 1, c).start()
-    lane = lax.broadcasted_iota(jnp.int32, (batch, LANES), 1)
-    low = lane < HEAD
+    pairs = ((q_hbm, q_buf), (k_hbm, k_buf), (len_hbm, lengths), (v_hbm, v_buf)) + tuple(zip(sources, targets))
+    copies = [pltpu.make_async_copy(source, target, sems.at[i]) for i, (source, target) in enumerate(pairs)]
+    for c in copies:
+        c.start()
+    low = lax.broadcasted_iota(jnp.int32, (batch, LANES), 1) < HEAD
+    spot = lax.broadcasted_iota(jnp.int32, (heads, context), 1) + lax.axis_index("kvp") * context
+    copies[0].wait()
     for h in range(heads):
-        wide = q_ref[:, (h // 2) * LANES : (h // 2 + 1) * LANES].astype(F32)
+        wide = q_buf[:, (h // 2) * LANES : (h // 2 + 1) * LANES].astype(F32)
         half = h // group
         if h % 2 != half:
             wide = pltpu.roll(wide, HEAD, 1)
         rows[h * batch : (h + 1) * batch, :] = jnp.where(low if half == 0 else ~low, wide, 0.0)
-    base = lax.axis_index("kvp") * context
-    spot = lax.broadcasted_iota(jnp.int32, (heads, context), 1)
-    slot = lax.broadcasted_iota(jnp.int32, (heads, LANES), 1)
-    mine = slot % heads == lax.broadcasted_iota(jnp.int32, (heads, LANES), 0)
-    field = slot // heads
     query = [rows[pl.ds(b, heads, stride=batch), :].astype(BF16) for b in range(batch)]
+    copies[1].wait()
+    scores = [
+        lax.dot_general(query[b], k_buf[b], (((1,), (1,)), ((), ())), preferred_element_type=F32)
+        for b in range(batch)
+    ]
+    copies[2].wait()
+    valid = [spot < lengths[b] for b in range(batch)]
+    masked = [jnp.where(valid[b], scores[b] * HEAD ** (-0.5), NEGATIVE) for b in range(batch)]
+    top = [jnp.max(masked[b], axis=1, keepdims=True) for b in range(batch)]
+    weights = [
+        jnp.where(valid[b], jnp.exp(masked[b] - top[b]), 0.0).astype(BF16) for b in range(batch)
+    ]
+    total = [jnp.sum(weights[b].astype(F32), axis=1, keepdims=True) for b in range(batch)]
+    copies[3].wait()
+    summed = [jnp.dot(weights[b], v_buf[b], preferred_element_type=F32) for b in range(batch)]
     for b in range(batch):
-        if b % step == 0:
-            copy(k_hbm, k_buf, 0, b // step).wait()
-            copy(v_hbm, v_buf, 1, b // step).wait()
-        scores = lax.dot_general(
-            query[b], k_buf[b], (((1,), (1,)), ((), ())), preferred_element_type=F32
-        ) * HEAD ** (-0.5)
-        valid = spot < len_ref[b] - base
-        masked = jnp.where(valid, scores, NEGATIVE)
-        top = jnp.max(masked, axis=1, keepdims=True)
-        weights = jnp.where(valid, jnp.exp(masked - top), 0.0).astype(BF16)
-        total = jnp.sum(weights.astype(F32), axis=1, keepdims=True)
-        summed = jnp.dot(weights, v_buf[b], preferred_element_type=F32)
-        rows[b * heads : (b + 1) * heads, :] = jnp.where(total > 0.0, summed / jnp.where(total > 0.0, total, 1.0), 0.0)
-        value = jnp.zeros((heads, LANES), F32)
-        for i, term in enumerate(split3(top) + split3(total)):
-            value = jnp.where(mine & (field == i), jnp.broadcast_to(term, (heads, LANES)), value)
-        stats[b : b + 1, :] = jnp.sum(value, axis=0, keepdims=True)
+        some = total[b] > 0.0
+        rows[b * heads : (b + 1) * heads, :] = summed[b] * jnp.where(some, 1.0 / jnp.where(some, total[b], 1.0), 0.0)
     for pair in range(heads // 2):
         sides = []
         for h in (2 * pair, 2 * pair + 1):
             wide = rows[pl.ds(h, batch, stride=heads), :]
             sides.append(pltpu.roll(wide, HEAD, 1) if h % 2 != h // group else wide)
         out_ref[:, pair * LANES : (pair + 1) * LANES] = jnp.where(low, sides[0], sides[1]).astype(BF16)
-    out_ref[:, heads * HEAD :] = stats[...].astype(BF16)
-
-
-def attention(queries, keys, values, lengths):
-    batch, context, width = keys.shape
+    slot = lax.broadcasted_iota(jnp.int32, (heads, LANES), 1)
+    mine = slot % heads == lax.broadcasted_iota(jnp.int32, (heads, LANES), 0)
+    field = [mine & (slot // heads == i) for i in range(6)]
+    for b in range(batch):
+        value = jnp.zeros((heads, LANES), F32)
+        for i, term in enumerate(split3(top[b]) + split3(total[b])):
+            value = jnp.where(field[i], jnp.broadcast_to(term, (heads, LANES)), value)
+        rows[b * heads : (b + 1) * heads, :] = value
+    pick = lax.broadcasted_iota(jnp.int32, (batch, batch * heads), 1) // heads == lax.broadcasted_iota(
+        jnp.int32, (batch, batch * heads), 0
+    )
+    stats = jnp.dot(
+        jnp.where(pick, 1.0, 0.0).astype(BF16), rows[...].astype(BF16), preferred_element_type=F32
+    )
+    out_ref[:, heads * HEAD :] = stats.astype(BF16)
+    for c in copies[4:]:
+        c.wait()
+
+
+def attention(queries, keys, values, lengths, weights):
+    batch, _, width = keys.shape
     heads = queries.shape[1] // HEAD
-    chunks = 4
     return pl.pallas_call(
-        functools.partial(attention_body, heads, width // HEAD, chunks),
-        out_shape=jax.ShapeDtypeStruct((batch, heads * HEAD + LANES), BF16),
-        in_specs=[SMEM, VMEM, ANY, ANY],
-        out_specs=VMEM,
+        functools.partial(attention_body, heads, width // HEAD, len(weights)),
+        out_shape=(
+            pltpu.VMEM((batch, heads * HEAD + LANES), BF16),
+            *(pltpu.VMEM(w.shape, w.dtype) for w in weights),
+        ),
+        in_specs=[HBM] * (4 + len(weights)),
+        out_specs=(VMEM,) * (1 + len(weights)),
         scratch_shapes=[
+            pltpu.SMEM(lengths.shape, jnp.int32),
+            pltpu.VMEM(queries.shape, BF16),
             pltpu.VMEM(keys.shape, BF16),
             pltpu.VMEM(values.shape, BF16),
             pltpu.VMEM((batch * heads, LANES), F32),
-            pltpu.VMEM((batch, LANES), F32),
-            pltpu.SemaphoreType.DMA((2, chunks)),
+            pltpu.SemaphoreType.DMA((4 + len(weights),)),
         ],
+        compiler_params=LIMIT,
         name="attention",
-    )(lengths, queries, keys, values)
+    )(*map(off_chip, (lengths, queries, keys, values, *weights)))
 
 
 def merge_body(heads, size, *refs):
@@ -151,13 +180,14 @@
     return pl.pallas_call(
         functools.partial(merge_body, inputs // HEAD, len(parts)),
         out_shape=(
-            jax.ShapeDtypeStruct((batch, inputs), F32),
-            jax.ShapeDtypeStruct((batch, columns), BF16),
+            pltpu.VMEM((batch, inputs), F32),
+            pltpu.VMEM((batch, columns), BF16),
         ),
         in_specs=[VMEM] * (len(parts) + 1),
         out_specs=(VMEM, VMEM),
+        compiler_params=LIMIT,
         name="merge",
-    )(*parts, weight)
+    )(*map(on_chip, (*parts, weight)))
 
 
 def state_body(size, *refs):
@@ -167,7 +197,7 @@
     state_ref[...] = state
     state = state.astype(F32)
     columns = state.shape[1]
-    out_ref[:, :columns] = (state * gain[...].astype(F32)).astype(BF16)
+    out_ref[:, :columns] = (state * gain[...].astype(F32).reshape(1, columns)).astype(BF16)
     squares = jnp.sum(state * state, axis=1, keepdims=True)
     lane = lax.broadcasted_iota(jnp.int32, (state.shape[0], LANES), 1)
     value = jnp.zeros(lane.shape, F32)
@@ -181,13 +211,14 @@
     return pl.pallas_call(
         functools.partial(state_body, len(parts)),
         out_shape=(
-            jax.ShapeDtypeStruct((batch, columns), BF16),
-            jax.ShapeDtypeStruct((batch, columns + LANES), BF16),
+            pltpu.VMEM((batch, columns), BF16),
+            pltpu.VMEM((batch, columns + LANES), BF16),
         ),
         in_specs=[VMEM] * (len(parts) + 2),
         out_specs=(VMEM, VMEM),
+        compiler_params=LIMIT,
         name="state",
-    )(*parts, residual, gain)
+    )(*map(on_chip, (*parts, residual, gain)))
 
 
 def expert_body(size, *refs):
@@ -208,7 +239,12 @@
         gate_sum, up_sum = gate_sum * inverse, up_sum * inverse
         hidden = (gate_sum / (1.0 + jnp.exp(-gate_sum)) * up_sum).astype(BF16)
         chosen = ids[...] == me * held + e
-        scale = jnp.sum(jnp.where(chosen, probs[...], 0.0), axis=1, keepdims=True)
+        across = jnp.sum(jnp.where(chosen, probs[...], 0.0), axis=0, keepdims=True)
+        batch = across.shape[1]
+        own = lax.broadcasted_iota(jnp.int32, (batch, batch), 0) == lax.broadcasted_iota(
+            jnp.int32, (batch, batch), 1
+        )
+        scale = jnp.sum(jnp.where(own, across, 0.0), axis=1, keepdims=True)
         for s in range(size):
             target = pl.ds(pl.multiple_of((me ^ s) * columns, LANES), columns)
             sums[s] += jnp.dot(hidden, down[e, :, target], preferred_element_type=F32) * scale
@@ -222,26 +258,27 @@
     columns = parts[0].shape[1] - LANES
     return pl.pallas_call(
         functools.partial(expert_body, size),
-        out_shape=tuple(jax.ShapeDtypeStruct((batch, columns), BF16) for _ in range(size)),
+        out_shape=tuple(pltpu.VMEM((batch, columns), BF16) for _ in range(size)),
         in_specs=[VMEM] * (size + 5),
         out_specs=(VMEM,) * size,
+        compiler_params=LIMIT,
         name="experts",
-    )(*parts, ids, probs, gate, up, down)
+    )(*map(on_chip, (*parts, ids.T, probs.T, gate, up, down)))
 
 
 def small_slice(
     queries, keys, values, lengths, out_weight, residual, norm_gain, expert_ids, gate_probs, w_gate, w_up, w_down
 ):
-    parts = exchange(attention(queries, keys, values, lengths), "kvp")
+    block, out_weight, w_gate, w_up, w_down = attention(
+        queries, keys, values, lengths, (out_weight, w_gate, w_up, w_down)
+    )
+    parts = share(block, "kvp")
     attended, projected = merge(parts, out_weight)
-    own_state, message = state(exchange(projected, "tp"), residual, norm_gain.reshape(1, -1))
-    outputs = experts(exchange(message, "kvp"), expert_ids, gate_probs, w_gate, w_up, w_down)
-    size = len(outputs)
-    moved = [outputs[0]] + [
-        lax.ppermute(outputs[s], "kvp", [(i, i ^ s) for i in range(size)]) for s in range(1, size)
-    ]
+    own_state, message = state(share(projected, "tp"), residual, norm_gain)
+    outputs = experts(share(message, "kvp"), expert_ids, gate_probs, w_gate, w_up, w_down)
+    moved = exchange(outputs, "kvp")
     owned = pairwise([m.astype(F32) for m in moved], add).astype(BF16)
-    moe_term = pairwise([m.astype(F32) for m in exchange(owned, "tp")], add)
+    moe_term = pairwise([m.astype(F32) for m in share(owned, "tp")], add)
     return attended, (own_state.astype(F32) + moe_term).astype(BF16)
 
 
@@ -321,7 +358,7 @@
     block_out = jnp.einsum(
         "bgrc,bcgd->bgrd", rounded, value_rows, preferred_element_type=jnp.float32
     )
-    global_max, denominator, summed = merged(
+    _, denominator, summed = merged(
         (block_max, block_sum, block_out), "kvp", merge_partial
     )
     attended = (summed / denominator[..., None]).reshape(batch_size, local_heads * HEAD)

time: 53.4 us -> 37.9 us (0.71)
  Pallas kernels: 14.2 us -> 3.97 us
  local copies, waits for them, and re-layouts: 3.77 us -> 0.65 us
  waiting for transfers between devices: 15.3 us -> 13.3 us
  other arithmetic: 1.33 us -> 0.63 us
  starting transfers between devices: 17.8 us -> 18.4 us
    pallas_call x3, Pallas kernels: 11.8 us -> 3.47 us  [the longest x1 2.65 us: attention(): pl.pallas_call(functools.partial(attention_body, heads, width // HEAD, le...]
    unnamed x28 -> x9, local copies, waits for them, and re-layouts: 3.18 us -> 0.65 us
    ppermute x15, waiting for transfers between devices: 15.3 us -> 13.3 us  [turn(): lax.ppermute(x, axis, [(i, i ^ s) for i in range(lax.axis_size(axis))])]
    pallas_call x1, Pallas kernels: 2.32 us -> 0.5 us  [merge(): pl.pallas_call(functools.partial(merge_body, inputs // HEAD, len(parts)),...]
    convert_element_type x1, other arithmetic: 0.72 us -> 0.01 us  [small_slice(): owned = pairwise([m.astype(F32) for m in moved], add).astype(BF16)]
    ppermute x15, starting transfers between devices: 17.8 us -> 18.4 us  [turn(): lax.ppermute(x, axis, [(i, i ^ s) for i in range(lax.axis_size(axis))])]
    reshape x1 -> x0, local copies, waits for them, and re-layouts: 0.6 us -> none  [small_slice(): norm_gain.reshape(1, -1)]
  transfers between devices with their start and end apart: 15 -> 15, of which waited for: 10 -> 11; matrix products, arithmetic and copies ran while one was open for 4% -> 2% of each run, Pallas kernels for 0% -> 0%
where the time goes in v2:
time: 37.9 us; the launch traced here: 37.7 us
  starting transfers between devices  18.4 us (49%)
  waiting for transfers between devices  13.3 us (35%)
  Pallas kernels  3.97 us (10%)
  between operations  0.71 us (2%)
  local copies, waits for them, and re-layouts  0.65 us (2%)
  other arithmetic  0.63 us (2%)
    ppermute x15, starting transfers between devices, turn(): lax.ppermute(x, axis, [(i, i ^ s) for i in range(lax.axis_size(axis))])  18.4 us
    ppermute x15, waiting for transfers between devices, turn(): lax.ppermute(x, axis, [(i, i ^ s) for i in range(lax.axis_size(axis))])  13.3 us
    pallas_call x1, Pallas kernels, attention(): pl.pallas_call(functools.partial(attention_body, heads, width // HEAD, le...  2.65 us
  transfers between devices with their start and end apart: 15, of which 11 were waited for; matrix products, arithmetic and copies ran while one was open for 2% of the time, Pallas kernels for 0%

profile of v2, /device:TPU:0, one launch (start us, length us, event | category | flops | bytes accessed | tf_op | source)
XLA Modules:
  0.0 37.7 jit_solution(7359082478690607795)
XLA Ops:
  0.6 0.0 copy-start.3
  0.6 0.0 copy-start
  0.7 0.0 copy-start.2
  0.7 0.0 copy-start.1
  0.7 2.6 %attention.1 = (bf16[16,1152]{1,0:T(8,128)(2,1)S(1)}, bf16[1024,384]{1,0:T(8,128)(2,1)S(1)}, bf16[1,1536,384]{2,1,0:T(8,128)(2,1)S(1)}, bf16[1,1536,384]{2,1,0:T(8,128)(2,1)S(1)}, bf16[1,384,1536]{2,1,0:T(8,128)(2,1)S(1)}) custom-call(s32[16]{0:T(128)} %refs_0_.1, bf16[16,1024]{1,0:T(8,128)(2,1)} %refs_1_.1, bf16[16,128,128]{2,1,0:T(8,128)(2,1)} %refs_2_.1, ...), custom_call_target="tpu_custom_call" | custom-call | tf_op jit(solution)/shard_map/attention/pallas_call | solution.py:127
  3.3 5.1 %collective-permute-start.2 = (bf16[16,1152]{1,0:T(8,128)(2,1)S(1)}, bf16[16,1152]{1,0:T(8,128)(2,1)S(1)}, u32[]{:S(2)}, u32[]{:S(2)}) collective-permute-start(bf16[16,1152]{1,0:T(8,128)(2,1)S(1)} %get-tuple-element.15.refs_0_), channel_id=1, source_target_pairs={{0,12},{4,8},{8,4},{12,0},{1,13},{5,9},{9,5},{13,1},{2,14},{6,10},... | collective-permute-start | bytes 110600 | tf_op jit(solution)/shard_map/ppermute | solution.py:23
  8.5 0.0 collective-permute-start.1
  8.5 0.6 %collective-permute-start = (bf16[16,1152]{1,0:T(8,128)(2,1)S(1)}, bf16[16,1152]{1,0:T(8,128)(2,1)S(1)}, u32[]{:S(2)}, u32[]{:S(2)}) collective-permute-start(bf16[16,1152]{1,0:T(8,128)(2,1)S(1)} %get-tuple-element.15.refs_0_), channel_id=1, source_target_pairs={{0,4},{4,0},{8,12},{12,8},{1,5},{5,1},{9,13},{13,9},{2,6},{6,2},{1... | collective-permute-start | bytes 110600 | tf_op jit(solution)/shard_map/ppermute | solution.py:23
  9.1 1.3 %collective-permute-done.2.refs_3_ = bf16[16,1152]{1,0:T(8,128)(2,1)S(1)} collective-permute-done((bf16[16,1152]{1,0:T(8,128)(2,1)S(1)}, bf16[16,1152]{1,0:T(8,128)(2,1)S(1)}, u32[]{:S(2)}, u32[]{:S(2)}) %collective-permute-start.2) | collective-permute-done | bytes 36896 | tf_op jit(solution)/shard_map/ppermute | solution.py:23
  10.4 2.9 %collective-permute-done.1.refs_2_ = bf16[16,1152]{1,0:T(8,128)(2,1)S(1)} collective-permute-done((bf16[16,1152]{1,0:T(8,128)(2,1)S(1)}, bf16[16,1152]{1,0:T(8,128)(2,1)S(1)}, u32[]{:S(2)}, u32[]{:S(2)}) %collective-permute-start.1) | collective-permute-done | bytes 36896 | tf_op jit(solution)/shard_map/ppermute | solution.py:23
  13.3 0.0 collective-permute-done.refs_1_
  13.3 0.5 %merge.1 = (f32[16,1024]{1,0:T(8,128)S(1)}, bf16[16,384]{1,0:T(8,128)(2,1)S(1)}) custom-call(bf16[16,1152]{1,0:T(8,128)(2,1)S(1)} %get-tuple-element.15.refs_0_, bf16[16,1152]{1,0:T(8,128)(2,1)S(1)} %collective-permute-done.refs_1_, bf16[16,1152]{1,0:T(8,128)(2,1)S(1)} %collective-permute-done.1.refs_2_, ...), custom_call_target="tpu_custom_call" | custom-call | tf_op jit(solution)/shard_map/merge/pallas_call | solution.py:180
  13.8 0.0 collective-permute-start.5
  13.8 1.5 %collective-permute-start.4 = (bf16[16,384]{1,0:T(8,128)(2,1)S(1)}, bf16[16,384]{1,0:T(8,128)(2,1)S(1)}, u32[]{:S(2)}, u32[]{:S(2)}) collective-permute-start(bf16[16,384]{1,0:T(8,128)(2,1)S(1)} %get-tuple-element.18.refs_0_), channel_id=1, source_target_pairs={{0,2},{1,3},{2,0},{3,1},{4,6},{5,7},{6,4},{7,5},{8,10},{9,11},{10,... | collective-permute-start | bytes 36872 | tf_op jit(solution)/shard_map/ppermute | solution.py:23
  15.4 0.3 collective-permute-start.3
  15.7 1.3 %collective-permute-done.5.refs_3_ = bf16[16,384]{1,0:T(8,128)(2,1)S(1)} collective-permute-done((bf16[16,384]{1,0:T(8,128)(2,1)S(1)}, bf16[16,384]{1,0:T(8,128)(2,1)S(1)}, u32[]{:S(2)}, u32[]{:S(2)}) %collective-permute-start.5) | collective-permute-done | bytes 12320 | tf_op jit(solution)/shard_map/ppermute | solution.py:23
  17.0 0.5 %collective-permute-done.4.refs_2_ = bf16[16,384]{1,0:T(8,128)(2,1)S(1)} collective-permute-done((bf16[16,384]{1,0:T(8,128)(2,1)S(1)}, bf16[16,384]{1,0:T(8,128)(2,1)S(1)}, u32[]{:S(2)}, u32[]{:S(2)}) %collective-permute-start.4) | collective-permute-done | bytes 12320 | tf_op jit(solution)/shard_map/ppermute | solution.py:23
  17.6 0.0 collective-permute-done.3.refs_1_
  17.6 0.0 copy-done.3
  17.6 0.0 copy-done
  17.6 0.1 state.1
  17.7 1.5 %collective-permute-start.8 = (bf16[16,512]{1,0:T(8,128)(2,1)S(1)}, bf16[16,512]{1,0:T(8,128)(2,1)S(1)}, u32[]{:S(2)}, u32[]{:S(2)}) collective-permute-start(bf16[16,512]{1,0:T(8,128)(2,1)S(1)} %get-tuple-element.20.refs_0_), channel_id=1, source_target_pairs={{0,12},{4,8},{8,4},{12,0},{1,13},{5,9},{9,5},{13,1},{2,14},{6,10},... | collective-permute-start | bytes 49160 | tf_op jit(solution)/shard_map/ppermute | solution.py:23
  19.2 0.6 %collective-permute-start.7 = (bf16[16,512]{1,0:T(8,128)(2,1)S(1)}, bf16[16,512]{1,0:T(8,128)(2,1)S(1)}, u32[]{:S(2)}, u32[]{:S(2)}) collective-permute-start(bf16[16,512]{1,0:T(8,128)(2,1)S(1)} %get-tuple-element.20.refs_0_), channel_id=1, source_target_pairs={{0,8},{4,12},{8,0},{12,4},{1,9},{5,13},{9,1},{13,5},{2,10},{6,14},... | collective-permute-start | bytes 49160 | tf_op jit(solution)/shard_map/ppermute | solution.py:23
  19.8 2.3 %collective-permute-start.6 = (bf16[16,512]{1,0:T(8,128)(2,1)S(1)}, bf16[16,512]{1,0:T(8,128)(2,1)S(1)}, u32[]{:S(2)}, u32[]{:S(2)}) collective-permute-start(bf16[16,512]{1,0:T(8,128)(2,1)S(1)} %get-tuple-element.20.refs_0_), channel_id=1, source_target_pairs={{0,4},{4,0},{8,12},{12,8},{1,5},{5,1},{9,13},{13,9},{2,6},{6,2},{1... | collective-permute-start | bytes 49160 | tf_op jit(solution)/shard_map/ppermute | solution.py:23
  22.1 1.1 %collective-permute-done.8.refs_3_ = bf16[16,512]{1,0:T(8,128)(2,1)S(1)} collective-permute-done((bf16[16,512]{1,0:T(8,128)(2,1)S(1)}, bf16[16,512]{1,0:T(8,128)(2,1)S(1)}, u32[]{:S(2)}, u32[]{:S(2)}) %collective-permute-start.8) | collective-permute-done | bytes 16416 | tf_op jit(solution)/shard_map/ppermute | solution.py:23
  23.2 0.6 %collective-permute-done.7.refs_2_ = bf16[16,512]{1,0:T(8,128)(2,1)S(1)} collective-permute-done((bf16[16,512]{1,0:T(8,128)(2,1)S(1)}, bf16[16,512]{1,0:T(8,128)(2,1)S(1)}, u32[]{:S(2)}, u32[]{:S(2)}) %collective-permute-start.7) | collective-permute-done | bytes 16416 | tf_op jit(solution)/shard_map/ppermute | solution.py:23
  23.8 0.2 collective-permute-done.6.refs_1_
  24.0 0.0 copy-done.2
  24.0 0.0 copy-done.1
  24.0 0.7 %experts.1 = (bf16[16,384]{1,0:T(8,128)(2,1)S(1)}, bf16[16,384]{1,0:T(8,128)(2,1)S(1)}, bf16[16,384]{1,0:T(8,128)(2,1)S(1)}, bf16[16,384]{1,0:T(8,128)(2,1)S(1)}) custom-call(bf16[16,512]{1,0:T(8,128)(2,1)S(1)} %get-tuple-element.20.refs_0_, bf16[16,512]{1,0:T(8,128)(2,1)S(1)} %collective-permute-done.6.refs_1_, ...), custom_call_target="tpu_custom_call" | custom-call | tf_op jit(solution)/shard_map/experts/pallas_call | solution.py:259
  24.7 1.9 %collective-permute-start.9 = (bf16[16,384]{1,0:T(8,128)(2,1)S(1)}, bf16[16,384]{1,0:T(8,128)(2,1)S(1)}, u32[]{:S(2)}, u32[]{:S(2)}) collective-permute-start(bf16[16,384]{1,0:T(8,128)(2,1)S(1)} %get-tuple-element.25), channel_id=1, source_target_pairs={{0,4},{4,0},{8,12},{12,8},{1,5},{5,1},{9,13},{13,9},{2,6},{6,2},{1... | collective-permute-start | bytes 36872 | tf_op jit(solution)/shard_map/ppermute | solution.py:23
  26.6 1.1 %collective-permute-start.10 = (bf16[16,384]{1,0:T(8,128)(2,1)S(1)}, bf16[16,384]{1,0:T(8,128)(2,1)S(1)}, u32[]{:S(2)}, u32[]{:S(2)}) collective-permute-start(bf16[16,384]{1,0:T(8,128)(2,1)S(1)} %get-tuple-element.26), channel_id=1, source_target_pairs={{0,8},{4,12},{8,0},{12,4},{1,9},{5,13},{9,1},{13,5},{2,10},{6,14},... | collective-permute-start | bytes 36872 | tf_op jit(solution)/shard_map/ppermute | solution.py:23
  27.7 1.4 %collective-permute-start.11 = (bf16[16,384]{1,0:T(8,128)(2,1)S(1)}, bf16[16,384]{1,0:T(8,128)(2,1)S(1)}, u32[]{:S(2)}, u32[]{:S(2)}) collective-permute-start(bf16[16,384]{1,0:T(8,128)(2,1)S(1)} %get-tuple-element.27), channel_id=1, source_target_pairs={{0,12},{4,8},{8,4},{12,0},{1,13},{5,9},{9,5},{13,1},{2,14},{6,10},... | collective-permute-start | bytes 36872 | tf_op jit(solution)/shard_map/ppermute | solution.py:23
  29.1 0.0 collective-permute-done.9
  29.1 2.1 %collective-permute-done.10 = bf16[16,384]{1,0:T(8,128)(2,1)S(1)} collective-permute-done((bf16[16,384]{1,0:T(8,128)(2,1)S(1)}, bf16[16,384]{1,0:T(8,128)(2,1)S(1)}, u32[]{:S(2)}, u32[]{:S(2)}) %collective-permute-start.10) | collective-permute-done | bytes 12320 | tf_op jit(solution)/shard_map/ppermute | solution.py:23
  31.2 2.0 %collective-permute-done.11 = bf16[16,384]{1,0:T(8,128)(2,1)S(1)} collective-permute-done((bf16[16,384]{1,0:T(8,128)(2,1)S(1)}, bf16[16,384]{1,0:T(8,128)(2,1)S(1)}, u32[]{:S(2)}, u32[]{:S(2)}) %collective-permute-start.11) | collective-permute-done | bytes 12320 | tf_op jit(solution)/shard_map/ppermute | solution.py:23
  33.2 0.1 collective-permute-start.14
  33.3 1.6 %collective-permute-start.13 = (bf16[16,384]{1,0:T(8,128)(2,1)S(1)}, bf16[16,384]{1,0:T(8,128)(2,1)S(1)}, u32[]{:S(2)}, u32[]{:S(2)}) collective-permute-start(bf16[16,384]{1,0:T(8,128)(2,1)S(1)} %add_convert_fusion.1), channel_id=1, source_target_pairs={{0,2},{1,3},{2,0},{3,1},{4,6},{5,7},{6,4},{7,5},{8,10},{9,11},{10,... | collective-permute-start | bytes 36872 | tf_op jit(solution)/shard_map/ppermute | solution.py:23
  34.9 0.3 collective-permute-start.12
  35.2 0.6 %copy.14 = f32[16,1024]{1,0:T(8,128)} copy(f32[16,1024]{1,0:T(8,128)S(1)} %get-tuple-element.28) | data formatting | bytes 131072
  35.8 0.7 %collective-permute-done.14 = bf16[16,384]{1,0:T(8,128)(2,1)S(1)} collective-permute-done((bf16[16,384]{1,0:T(8,128)(2,1)S(1)}, bf16[16,384]{1,0:T(8,128)(2,1)S(1)}, u32[]{:S(2)}, u32[]{:S(2)}) %collective-permute-start.14) | collective-permute-done | bytes 12320 | tf_op jit(solution)/shard_map/ppermute | solution.py:23
  36.5 0.6 %collective-permute-done.13 = bf16[16,384]{1,0:T(8,128)(2,1)S(1)} collective-permute-done((bf16[16,384]{1,0:T(8,128)(2,1)S(1)}, bf16[16,384]{1,0:T(8,128)(2,1)S(1)}, u32[]{:S(2)}, u32[]{:S(2)}) %collective-permute-start.13) | collective-permute-done | bytes 12320 | tf_op jit(solution)/shard_map/ppermute | solution.py:23
  37.1 0.0 collective-permute-done.12
  37.1 0.6 %add_convert_fusion = bf16[16,384]{1,0:T(8,128)(2,1)} fusion(bf16[16,384]{1,0:T(8,128)(2,1)S(1)} %collective-permute-done.14, bf16[16,384]{1,0:T(8,128)(2,1)S(1)} %collective-permute-done.13, bf16[16,384]{1,0:T(8,128)(2,1)S(1)} %collective-permute-done.12, bf16[16,384]{1,0:T(8,128)(2,1)S(1)} %add_convert_fusion.1, bf16[16,384]{1,0:T(8,128)(2,1)S(1)} %get-tuple-element.19), kind=kLoop, calls=%fused_computation | loop fusion | flops 61440 | bytes 73728 | tf_op jit(solution)/shard_map/convert_element_type | solution.py:282
  (1 shorter events, 0.0 us)
Async XLA Ops:
  0.6 17.0 %copy-start.3 = (bf16[384]{0:T(512)(128)(2,1)S(1)}, bf16[384]{0:T(512)(128)(2,1)}, u32[]{:S(2)}) copy-start(bf16[384]{0:T(512)(128)(2,1)} %refs_5_.3) | copy-start | bytes 2308
  0.6 16.9 %copy-start = (bf16[16,384]{1,0:T(8,128)(2,1)S(1)}, bf16[16,384]{1,0:T(8,128)(2,1)}, u32[]{:S(2)}) copy-start(bf16[16,384]{1,0:T(8,128)(2,1)} %refs_4_.3) | copy-start | bytes 36868
  0.7 23.3 %copy-start.2 = (f32[16,4]{0,1:T(4,128)S(1)}, f32[16,4]{0,1:T(4,128)}, u32[]{:S(2)}) copy-start(f32[16,4]{0,1:T(4,128)} %param.20) | copy-start | bytes 772
  0.7 23.3 %copy-start.1 = (s32[16,4]{0,1:T(4,128)S(1)}, s32[16,4]{0,1:T(4,128)}, u32[]{:S(2)}) copy-start(s32[16,4]{0,1:T(4,128)} %param.19) | copy-start | bytes 772
  3.3 7.1 %collective-permute-start.2 = (bf16[16,1152]{1,0:T(8,128)(2,1)S(1)}, bf16[16,1152]{1,0:T(8,128)(2,1)S(1)}, u32[]{:S(2)}, u32[]{:S(2)}) collective-permute-start(bf16[16,1152]{1,0:T(8,128)(2,1)S(1)} %get-tuple-element.15.refs_0_), channel_id=1, source_target_pairs={{0,12},{4,8},{8,4},{12,0},{1,13},{5,9},{9,5},{13,1},{2,14},{6,10},... | collective-permute-start | bytes 110600 | tf_op jit(solution)/shard_map/ppermute | solution.py:23
  8.5 4.9 %collective-permute-start.1 = (bf16[16,1152]{1,0:T(8,128)(2,1)S(1)}, bf16[16,1152]{1,0:T(8,128)(2,1)S(1)}, u32[]{:S(2)}, u32[]{:S(2)}) collective-permute-start(bf16[16,1152]{1,0:T(8,128)(2,1)S(1)} %get-tuple-element.15.refs_0_), channel_id=1, source_target_pairs={{0,8},{4,12},{8,0},{12,4},{1,9},{5,13},{9,1},{13,5},{2,10},{6,14},... | collective-permute-start | bytes 110600 | tf_op jit(solution)/shard_map/ppermute | solution.py:23
  8.5 4.9 %collective-permute-start = (bf16[16,1152]{1,0:T(8,128)(2,1)S(1)}, bf16[16,1152]{1,0:T(8,128)(2,1)S(1)}, u32[]{:S(2)}, u32[]{:S(2)}) collective-permute-start(bf16[16,1152]{1,0:T(8,128)(2,1)S(1)} %get-tuple-element.15.refs_0_), channel_id=1, source_target_pairs={{0,4},{4,0},{8,12},{12,8},{1,5},{5,1},{9,13},{13,9},{2,6},{6,2},{1... | collective-permute-start | bytes 110600 | tf_op jit(solution)/shard_map/ppermute | solution.py:23
  13.8 3.2 %collective-permute-start.5 = (bf16[16,384]{1,0:T(8,128)(2,1)S(1)}, bf16[16,384]{1,0:T(8,128)(2,1)S(1)}, u32[]{:S(2)}, u32[]{:S(2)}) collective-permute-start(bf16[16,384]{1,0:T(8,128)(2,1)S(1)} %get-tuple-element.18.refs_0_), channel_id=1, source_target_pairs={{0,3},{1,2},{2,1},{3,0},{4,7},{5,6},{6,5},{7,4},{8,11},{9,10},{10,... | collective-permute-start | bytes 36872 | tf_op jit(solution)/shard_map/ppermute | solution.py:23
  13.8 3.8 %collective-permute-start.4 = (bf16[16,384]{1,0:T(8,128)(2,1)S(1)}, bf16[16,384]{1,0:T(8,128)(2,1)S(1)}, u32[]{:S(2)}, u32[]{:S(2)}) collective-permute-start(bf16[16,384]{1,0:T(8,128)(2,1)S(1)} %get-tuple-element.18.refs_0_), channel_id=1, source_target_pairs={{0,2},{1,3},{2,0},{3,1},{4,6},{5,7},{6,4},{7,5},{8,10},{9,11},{10,... | collective-permute-start | bytes 36872 | tf_op jit(solution)/shard_map/ppermute | solution.py:23
  15.4 2.2 %collective-permute-start.3 = (bf16[16,384]{1,0:T(8,128)(2,1)S(1)}, bf16[16,384]{1,0:T(8,128)(2,1)S(1)}, u32[]{:S(2)}, u32[]{:S(2)}) collective-permute-start(bf16[16,384]{1,0:T(8,128)(2,1)S(1)} %get-tuple-element.18.refs_0_), channel_id=1, source_target_pairs={{0,1},{1,0},{2,3},{3,2},{4,5},{5,4},{6,7},{7,6},{8,9},{9,8},{10,11... | collective-permute-start | bytes 36872 | tf_op jit(solution)/shard_map/ppermute | solution.py:23
  17.7 5.5 %collective-permute-start.8 = (bf16[16,512]{1,0:T(8,128)(2,1)S(1)}, bf16[16,512]{1,0:T(8,128)(2,1)S(1)}, u32[]{:S(2)}, u32[]{:S(2)}) collective-permute-start(bf16[16,512]{1,0:T(8,128)(2,1)S(1)} %get-tuple-element.20.refs_0_), channel_id=1, source_target_pairs={{0,12},{4,8},{8,4},{12,0},{1,13},{5,9},{9,5},{13,1},{2,14},{6,10},... | collective-permute-start | bytes 49160 | tf_op jit(solution)/shard_map/ppermute | solution.py:23
  19.2 4.6 %collective-permute-start.7 = (bf16[16,512]{1,0:T(8,128)(2,1)S(1)}, bf16[16,512]{1,0:T(8,128)(2,1)S(1)}, u32[]{:S(2)}, u32[]{:S(2)}) collective-permute-start(bf16[16,512]{1,0:T(8,128)(2,1)S(1)} %get-tuple-element.20.refs_0_), channel_id=1, source_target_pairs={{0,8},{4,12},{8,0},{12,4},{1,9},{5,13},{9,1},{13,5},{2,10},{6,14},... | collective-permute-start | bytes 49160 | tf_op jit(solution)/shard_map/ppermute | solution.py:23
  19.8 4.2 %collective-permute-start.6 = (bf16[16,512]{1,0:T(8,128)(2,1)S(1)}, bf16[16,512]{1,0:T(8,128)(2,1)S(1)}, u32[]{:S(2)}, u32[]{:S(2)}) collective-permute-start(bf16[16,512]{1,0:T(8,128)(2,1)S(1)} %get-tuple-element.20.refs_0_), channel_id=1, source_target_pairs={{0,4},{4,0},{8,12},{12,8},{1,5},{5,1},{9,13},{13,9},{2,6},{6,2},{1... | collective-permute-start | bytes 49160 | tf_op jit(solution)/shard_map/ppermute | solution.py:23
  24.7 4.4 %collective-permute-start.9 = (bf16[16,384]{1,0:T(8,128)(2,1)S(1)}, bf16[16,384]{1,0:T(8,128)(2,1)S(1)}, u32[]{:S(2)}, u32[]{:S(2)}) collective-permute-start(bf16[16,384]{1,0:T(8,128)(2,1)S(1)} %get-tuple-element.25), channel_id=1, source_target_pairs={{0,4},{4,0},{8,12},{12,8},{1,5},{5,1},{9,13},{13,9},{2,6},{6,2},{1... | collective-permute-start | bytes 36872 | tf_op jit(solution)/shard_map/ppermute | solution.py:23
  26.6 4.6 %collective-permute-start.10 = (bf16[16,384]{1,0:T(8,128)(2,1)S(1)}, bf16[16,384]{1,0:T(8,128)(2,1)S(1)}, u32[]{:S(2)}, u32[]{:S(2)}) collective-permute-start(bf16[16,384]{1,0:T(8,128)(2,1)S(1)} %get-tuple-element.26), channel_id=1, source_target_pairs={{0,8},{4,12},{8,0},{12,4},{1,9},{5,13},{9,1},{13,5},{2,10},{6,14},... | collective-permute-start | bytes 36872 | tf_op jit(solution)/shard_map/ppermute | solution.py:23
  27.7 5.5 %collective-permute-start.11 = (bf16[16,384]{1,0:T(8,128)(2,1)S(1)}, bf16[16,384]{1,0:T(8,128)(2,1)S(1)}, u32[]{:S(2)}, u32[]{:S(2)}) collective-permute-start(bf16[16,384]{1,0:T(8,128)(2,1)S(1)} %get-tuple-element.27), channel_id=1, source_target_pairs={{0,12},{4,8},{8,4},{12,0},{1,13},{5,9},{9,5},{13,1},{2,14},{6,10},... | collective-permute-start | bytes 36872 | tf_op jit(solution)/shard_map/ppermute | solution.py:23
  33.2 3.3 %collective-permute-start.14 = (bf16[16,384]{1,0:T(8,128)(2,1)S(1)}, bf16[16,384]{1,0:T(8,128)(2,1)S(1)}, u32[]{:S(2)}, u32[]{:S(2)}) collective-permute-start(bf16[16,384]{1,0:T(8,128)(2,1)S(1)} %add_convert_fusion.1), channel_id=1, source_target_pairs={{0,3},{1,2},{2,1},{3,0},{4,7},{5,6},{6,5},{7,4},{8,11},{9,10},{10,... | collective-permute-start | bytes 36872 | tf_op jit(solution)/shard_map/ppermute | solution.py:23
  33.3 3.8 %collective-permute-start.13 = (bf16[16,384]{1,0:T(8,128)(2,1)S(1)}, bf16[16,384]{1,0:T(8,128)(2,1)S(1)}, u32[]{:S(2)}, u32[]{:S(2)}) collective-permute-start(bf16[16,384]{1,0:T(8,128)(2,1)S(1)} %add_convert_fusion.1), channel_id=1, source_target_pairs={{0,2},{1,3},{2,0},{3,1},{4,6},{5,7},{6,4},{7,5},{8,10},{9,11},{10,... | collective-permute-start | bytes 36872 | tf_op jit(solution)/shard_map/ppermute | solution.py:23
  34.9 2.2 %collective-permute-start.12 = (bf16[16,384]{1,0:T(8,128)(2,1)S(1)}, bf16[16,384]{1,0:T(8,128)(2,1)S(1)}, u32[]{:S(2)}, u32[]{:S(2)}) collective-permute-start(bf16[16,384]{1,0:T(8,128)(2,1)S(1)} %add_convert_fusion.1), channel_id=1, source_target_pairs={{0,1},{1,0},{2,3},{3,2},{4,5},{5,4},{6,7},{7,6},{8,9},{9,8},{10,11... | collective-permute-start | bytes 36872 | tf_op jit(solution)/shard_map/ppermute | solution.py:23
